TPU v7x, 32 devices: a whole 2x2x4 slice. The times are simulated.
32 devices in a mesh: dp: 16 (over z, y, x), mp: 2 (over core).
Axes of the slice: x: 2, y: 2, z: 4, core: 2. Of those that a mesh axis runs over, the one named last changes fastest.
Arguments:
- residual_input: bfloat16 [4096, 5120], P('dp', 'mp'), may hold values from -6 to 6
- cotangent: bfloat16 [4096, 5120], P('dp', 'mp'), may hold values from -0.6 to 0.6
- lengths: int32 [16], P('dp'), may hold values from 64 to 256
- norm_gain_vector: bfloat16 [5120], replicated, may hold values from 0.5 to 1.5
- gate_projection_weight: bfloat16 [5120, 6912], P('dp', 'mp'), may hold values from -0.078125 to 0.078125
- up_projection_weight: bfloat16 [5120, 6912], P('dp', 'mp'), may hold values from -0.078125 to 0.078125
- down_projection_weight: bfloat16 [5120, 6912], P('dp', 'mp'), may hold values from -0.078125 to 0.078125
- up_adapter_first: bfloat16 [5120, 16], replicated, may hold values from -0.078125 to 0.078125
- up_adapter_second: bfloat16 [16, 6912], P(None, 'mp'), may hold values from -0.29882812 to 0.29882812
- down_adapter_first: bfloat16 [6912, 16], P('mp'), may hold values from -0.078125 to 0.078125
- down_adapter_second: bfloat16 [16, 5120], replicated, may hold values from -0.29882812 to 0.29882812
Outputs:
- up_first_gradient: float32 [5120, 16], P('dp')
- up_second_gradient: float32 [16, 6912], P(None, ('mp', 'dp'))
- down_first_gradient: float32 [6912, 16], P(('mp', 'dp'))
- down_second_gradient: float32 [16, 5120], P(None, 'dp')
All inputs are finite; a program needn't handle non-finite values.
Results may differ from a plain program's by a relative error of at most 0.0061.
Values may be sent and summed in bfloat16 or wider, within the bound.
No kernel may reach another device: no remote copies, remote signals or barrier semaphores. Data moves between devices by JAX's collectives and lax.ppermute only.
A program may use at most 192 MiB of HBM per device.

v0:
```python
import math

import jax
import jax.numpy as jnp
from jax import lax
from jax.experimental import pallas as pl
from jax.experimental.pallas import tpu as pltpu
from jax.sharding import Mesh, PartitionSpec as P

norm_eps = 1e-06
adapter_scale = 2.0
clip_coefficient = 0.005


def matmul(left, right):
    return jnp.dot(left, right, preferred_element_type=jnp.float32)


def contract(left, right, left_dim, right_dim):
    return lax.dot_general(
        left, right, (((left_dim,), (right_dim,)), ((), ())), preferred_element_type=jnp.float32
    )


def outer_count(dp):
    return min(r for r in range(1, dp + 1) if dp % r == 0 and r * r >= dp)


def after(value, done):
    return lax.optimization_barrier((value, done))[0]


def copied(shape, places, arrays, plan, into=None):
    count = len(arrays)

    def kernel(place, *refs):
        sources, target, staged = refs[:count], refs[-count - 3], refs[-count - 2 : -2]
        loads = [
            pltpu.make_async_copy(source, stage, refs[-2].at[k])
            for k, (source, stage) in enumerate(zip(sources, staged))
        ]
        stores = [
            pltpu.make_async_copy(stage, to, refs[-1].at[k])
            for k, (stage, to) in enumerate(zip(staged, plan(place, target)))
        ]
        for load in loads:
            load.start()
        for load, store in zip(loads, stores):
            load.wait()
            store.start()
        for store in stores:
            store.wait()

    anywhere = pl.BlockSpec(memory_space=pl.ANY)
    extra = [] if into is None else [into]
    return pl.pallas_call(
        kernel,
        out_shape=jax.ShapeDtypeStruct(shape, arrays[0].dtype),
        in_specs=[pl.BlockSpec(memory_space=pltpu.SMEM)] + [anywhere] * (count + len(extra)),
        out_specs=anywhere,
        scratch_shapes=[pltpu.VMEM(a.shape, a.dtype) for a in arrays]
        + [pltpu.SemaphoreType.DMA((count,)), pltpu.SemaphoreType.DMA((count,))],
        input_output_aliases={} if into is None else {1 + count: 0},
    )(places, *arrays, *extra)


def column_pieces(weight, r):
    o = lax.axis_index("o")
    rows, width = weight.shape[0], weight.shape[1] // r
    return [lax.dynamic_slice(weight, (0, (o + d) % r * width), (rows, width)) for d in range(r)]


def exchange(pieces, r):
    return [pieces[0]] + [
        lax.ppermute(pieces[d], "o", [(s, (s + d) % r) for s in range(r)]) for d in range(1, r)
    ]


def by_position(got, r):
    o = lax.axis_index("o")
    places = (o - jnp.arange(r, dtype=jnp.int32)) % r
    return copied(
        (r,) + got[0].shape,
        places,
        got,
        lambda place, target: [target.at[place[d]] for d in range(r)],
    )


def neighbours(part, p):
    if p != 4:
        return [lax.all_gather(part, "i", axis=1)], []
    half = part.shape[0] // 2
    near = [lax.ppermute(part, "i", [(s, s ^ bit) for s in range(p)]) for bit in (1, 2)]
    return near, [near[0][:half], near[1][half:]]


def assembled(part, near, passed, p):
    if p != 4:
        return near[0].reshape(-1, part.shape[-1])
    half = part.shape[0] // 2
    places = lax.axis_index("i") ^ jnp.arange(p, dtype=jnp.int32)
    shape = (part.shape[0], p) + part.shape[1:]
    corner = [
        lax.ppermute(piece, "i", [(s, s ^ bit) for s in range(p)]) for piece, bit in zip(passed, (2, 1))
    ]
    out = copied(
        shape,
        places,
        [part] + near,
        lambda place, target: [target.at[:, place[k]] for k in range(3)],
    )
    out = copied(
        shape,
        places,
        corner,
        lambda place, target: [target.at[:half, place[3]], target.at[half:, place[3]]],
        out,
    )
    return out.reshape(-1, part.shape[-1])


def arrival(at, n, r):
    sides = list(range(at + 1, r)), list(range(at - 1, -1, -1))
    first, second = sides if at < r // 2 else sides[::-1]
    return ([at] + first + second)[n]


def gather_path(half, r):
    o = lax.axis_index("o")
    up, down = [half], [half]
    for k in range(1, r):
        up.append(lax.ppermute(up[-1], "o", [(s, s + 1) for s in range(k - 1, r - 1)]))
        down.append(lax.ppermute(down[-1], "o", [(s, s - 1) for s in range(1, r - k + 1)]))
    blocks = [half]
    for n in range(1, r):
        values = []
        for at in range(r):
            source = arrival(at, n, r)
            values.append(up[at - source] if source < at else down[source - at])
        distinct = list({id(v): v for v in values}.values())
        fenced = dict(zip(map(id, distinct), lax.optimization_barrier(distinct)))
        block = fenced[id(values[0])]
        for at in range(1, r):
            if values[at] is not values[at - 1]:
                block = jnp.where(o >= at, fenced[id(values[at])], block)
        blocks.append(block)
    return blocks, (up[1], down[1])


def across(block, mp):
    width = block.shape[1] // 2
    if mp != 2:
        both = lax.all_gather(block, "mp", axis=0)
        whole = lambda a: a.swapaxes(0, 1).reshape(block.shape[0], -1)
        return whole(both[:, :, :width]), whole(both[:, :, width:])
    other = lax.ppermute(block, "mp", [(0, 1), (1, 0)])
    first = lax.axis_index("mp") == 0
    south, north = jnp.where(first, block, other), jnp.where(first, other, block)
    return (
        jnp.concatenate([south[:, :width], north[:, :width]], axis=1),
        jnp.concatenate([south[:, width:], north[:, width:]], axis=1),
    )


def per_device(
    residual_input,
    cotangent,
    lengths,
    norm_gain_vector,
    gate_projection_weight,
    up_projection_weight,
    down_projection_weight,
    up_adapter_first,
    up_adapter_second,
    down_adapter_first,
    down_adapter_second,
    r,
    p,
):
    f32, bf16 = jnp.float32, jnp.bfloat16
    c, o = lax.axis_index("mp"), lax.axis_index("o")
    seq, part = residual_input.shape
    model_width, rank = up_adapter_first.shape
    mp = model_width // part
    block = model_width // (r * p)
    hidden = up_adapter_second.shape[1] // r
    clip_limit = clip_coefficient * math.sqrt(2.0 * rank * (model_width + hidden * r * mp))

    gate_cut = column_pieces(gate_projection_weight, r)
    up_cut = column_pieces(up_projection_weight, r)
    down_cut = column_pieces(down_projection_weight, r)

    wide = after(residual_input, gate_cut).astype(f32)
    mean = lax.psum(jnp.sum(wide * wide, axis=1, keepdims=True), "mp") / model_width
    gain = lax.dynamic_slice(norm_gain_vector, (c * part,), (part,)).astype(f32)
    normed = (wide * lax.rsqrt(mean + norm_eps) * gain).astype(bf16)
    live = (lax.broadcasted_iota(jnp.int32, (seq, 1), 0) < lengths[0]).astype(f32)
    grad_out = (cotangent.astype(f32) * live).astype(bf16)

    tokens, first_tokens = gather_path(jnp.concatenate([normed, grad_out], axis=1), r)
    gate_part = by_position(exchange(gate_cut, r), r)
    gate_near, gate_pass = neighbours(gate_part, p)
    up_part = by_position(exchange(up_cut, r), r)
    up_near, up_pass = neighbours(up_part, p)
    down_got = exchange(down_cut, r)
    down_part = by_position(after(down_got, (gate_pass, up_pass, first_tokens)), r)
    down_near, down_pass = neighbours(down_part, p)
    gate_weight = assembled(gate_part, gate_near, gate_pass, p)
    up_weight = assembled(up_part, up_near, up_pass, p)
    down_weight = assembled(down_part, down_near, down_pass, p)
    normed, grad_out = zip(*[across(t, mp) for t in tokens])
    table = jnp.array([[arrival(at, n, r) for n in range(r)] for at in range(r)], jnp.int32)
    places = lax.dynamic_index_in_dim(table, o, 0, keepdims=False)

    up_second = lax.dynamic_slice(up_adapter_second, (0, o * hidden), (rank, hidden))
    down_first = lax.dynamic_slice(down_adapter_first, (o * hidden, 0), (hidden, rank))

    def square(array):
        return jnp.sum(array * array)

    def cut(array, k, group, axis):
        at = group.index(k) * seq
        return lax.slice_in_dim(array, at, at + seq, axis=axis)

    lat, act, hid = {}, {}, {}
    for group in [[k] for k in range(r)]:
        n = jnp.concatenate([normed[k] for k in group], axis=0)
        group_lat = contract(up_adapter_first, n, 0, 1).astype(bf16)
        group_act = jax.nn.silu(matmul(n, gate_weight))
        up = matmul(n, up_weight) + adapter_scale * contract(group_lat, up_second, 0, 0)
        group_hid = (group_act * up).astype(bf16)
        for k in group:
            lat[k] = cut(group_lat, k, group, 1)
            act[k] = cut(group_act, k, group, 0)
            hid[k] = cut(group_hid, k, group, 0)

    sums = jnp.zeros((2 * rank + 2, r * seq), bf16)
    grad_up_second, grad_down_first = [], []
    for group in [[k] for k in range(r)]:
        g = jnp.concatenate([grad_out[k] for k in group], axis=0)
        back = contract(down_adapter_second, g, 1, 1).astype(bf16)
        grad_hidden = matmul(g, down_weight) + adapter_scale * contract(back, down_first, 0, 1)
        grad_up = jnp.concatenate([act[k] for k in group], axis=0) * grad_hidden
        grad_up = grad_up.astype(bf16)
        up_lat = contract(up_second, grad_up, 1, 1)
        for k in group:
            grad_down_first.append(adapter_scale * matmul(cut(back, k, group, 1), hid[k]))
            grad_up_second.append(adapter_scale * matmul(lat[k], cut(grad_up, k, group, 0)))
            split = square(grad_down_first[k]) + square(grad_up_second[k])
            high = split.astype(bf16)
            low = (split - high.astype(f32)).astype(bf16)
            partial = [
                contract(down_first, hid[k], 0, 1).astype(bf16),
                cut(up_lat, k, group, 1).astype(bf16),
                jnp.broadcast_to(high, (1, seq)),
                jnp.broadcast_to(low, (1, seq)),
            ]
            partial = jnp.concatenate(partial, axis=0)
            sums = lax.dynamic_update_slice(sums, partial, (0, places[k] * seq))

    products = []
    for tokens in (grad_out, normed):
        for t in tokens:
            products.append(contract(t, t, 1, 1))
    products = jnp.stack(lax.optimization_barrier(products))
    share = lambda t: lax.dynamic_slice(t, (0, o * p * block), (seq, p * block))
    grad_share = jnp.concatenate([share(g) for g in grad_out], axis=0)
    normed_share = jnp.concatenate([share(n) for n in normed], axis=0)

    sums = jnp.sum(lax.all_gather(sums, ("o", "mp"), axis=0).astype(f32), axis=0)
    sums = jnp.concatenate(
        [lax.dynamic_slice(sums, (0, places[k] * seq), (2 * rank + 2, seq)) for k in range(r)], axis=1
    )
    lat_down = sums[:rank].astype(bf16).astype(f32)
    up_lat = sums[rank : 2 * rank].astype(bf16).astype(f32)
    latents = jnp.concatenate([lat_down, up_lat], axis=1).reshape(rank, 2 * r, seq).swapaxes(0, 1)
    through = lax.dot_general(
        latents, products, (((2,), (1,)), ((0,), (0,))), precision=lax.Precision.HIGHEST
    )
    squares = adapter_scale**2 * jnp.sum(latents * through, axis=(1, 2)).reshape(2, r).sum(axis=0)
    squares = squares + sums[2 * rank, ::seq] + sums[2 * rank + 1, ::seq]
    factors = jnp.minimum(1.0, clip_limit / (jnp.sqrt(squares) + 1e-06))

    def clipped(arrays):
        return sum(factors[k] * array for k, array in enumerate(arrays))

    by_token = jnp.repeat(adapter_scale * factors, seq)[None]

    def token_gradient(latent, tokens):
        scaled = by_token * latent
        high = scaled.astype(bf16)
        low = (scaled - high.astype(f32)).astype(bf16)
        both = matmul(jnp.concatenate([high, low], axis=0), tokens)
        return both[:rank] + both[rank:]

    sizes = (block, hidden // p, hidden // p, block)
    pieces = (
        token_gradient(up_lat, normed_share),
        clipped(grad_up_second),
        clipped(grad_down_first),
        token_gradient(lat_down, grad_share),
    )
    pieces = [a.reshape(rank, p, size).swapaxes(0, 1) for a, size in zip(pieces, sizes)]
    pieces = jnp.concatenate(pieces, axis=2).astype(bf16)
    total = lax.all_to_all(pieces, "i", 0, 0, tiled=True)
    total = jnp.sum(total.reshape(p, rank, -1).astype(f32), axis=0)
    outs, start = [], 0
    for size in sizes:
        outs.append(total[:, start : start + size])
        start += size
    return outs[0].T, outs[1], outs[2].T, outs[3]


def solution(mesh):
    dp, mp = mesh.shape["dp"], mesh.shape["mp"]
    r = outer_count(dp)
    p = dp // r
    grid = Mesh(mesh.devices.reshape(r, p, mp), ("o", "i", "mp"))
    rows = ("o", "i")

    def body(*args):
        return per_device(*args, r=r, p=p)

    return jax.shard_map(
        body,
        mesh=grid,
        in_specs=(
            P(rows, "mp"),
            P(rows, "mp"),
            P(rows),
            P(),
            P(rows, "mp"),
            P(rows, "mp"),
            P(rows, "mp"),
            P(),
            P(None, "mp"),
            P("mp", None),
            P(),
        ),
        out_specs=(P(rows, None), P(None, ("mp", "o", "i")), P(("mp", "o", "i"), None), P(None, rows)),
        check_vma=False,
    )
```

profile of v0, /device:TPU:0, one launch (start us, length us, event | category | flops | bytes accessed | tf_op | source)
XLA Modules:
  0.0 582.9 jit_solution(10369794006533346411)
XLA Ops:
  1.5 4.4 constant_dynamic-slice_fusion.14
  14.1 6.9 %collective-permute-start.18 = (bf16[256,5120]{1,0:T(8,128)(2,1)}, bf16[256,5120]{1,0:T(8,128)(2,1)}, u32[]{:S(2)}, u32[]{:S(2)}) collective-permute-start(bf16[256,5120]{1,0:T(8,128)(2,1)} %pad_maximum_fusion.8), channel_id=1, source_target_pairs={{0,8},{8,16},{16,24},{1,9},{9,17},{17,25},{2,10},{10,18},{18,26},{... | collective-permute-start | bytes 7864328 | tf_op jit(solution)/shard_map/ppermute | solution.py:133
  28.1 61.3 %collective-permute-done.3.refs_3_ = bf16[320,864]{1,0:T(8,128)(2,1)S(1)} collective-permute-done((bf16[320,864]{1,0:T(8,128)(2,1)S(1)}, bf16[320,864]{1,0:T(8,128)(2,1)S(1)}, u32[]{:S(2)}, u32[]{:S(2)}) %collective-permute-start.3) | collective-permute-done | bytes 552992 | tf_op jit(solution)/shard_map/ppermute | solution.py:75
  89.9 11.8 %collective-permute-done.10.refs_3_ = bf16[320,864]{1,0:T(8,128)(2,1)} collective-permute-done((bf16[320,864]{1,0:T(8,128)(2,1)S(1)}, bf16[320,864]{1,0:T(8,128)(2,1)}, u32[]{:S(2)}, u32[]{:S(2)}) %collective-permute-start.10) | collective-permute-done | bytes 552992 | tf_op jit(solution)/shard_map/ppermute | solution.py:75
  103.3 11.8 %collective-permute-done.8.refs_1_ = bf16[320,864]{1,0:T(8,128)(2,1)} collective-permute-done((bf16[320,864]{1,0:T(8,128)(2,1)}, bf16[320,864]{1,0:T(8,128)(2,1)}, u32[]{:S(2)}, u32[]{:S(2)}) %collective-permute-start.8) | collective-permute-done | bytes 552992 | tf_op jit(solution)/shard_map/ppermute | solution.py:75
  116.5 46.8 %collective-permute-done.9.refs_2_ = bf16[320,864]{1,0:T(8,128)(2,1)} collective-permute-done((bf16[320,864]{1,0:T(8,128)(2,1)}, bf16[320,864]{1,0:T(8,128)(2,1)}, u32[]{:S(2)}, u32[]{:S(2)}) %collective-permute-start.9) | collective-permute-done | bytes 552992 | tf_op jit(solution)/shard_map/ppermute | solution.py:75
  168.3 4.3 constant_dynamic-slice_fusion.5
  193.0 39.6 %collective-permute-done.13.refs_2_ = bf16[4,320,864]{2,1,0:T(8,128)(2,1)} collective-permute-done((bf16[4,320,864]{2,1,0:T(8,128)(2,1)}, bf16[4,320,864]{2,1,0:T(8,128)(2,1)}, u32[]{:S(2)}, u32[]{:S(2)}) %collective-permute-start.13) | collective-permute-done | bytes 2211872 | tf_op jit(solution)/shard_map/ppermute | solution.py:94
  239.6 40.2 %collective-permute-done.6.refs_2_ = bf16[4,320,864]{2,1,0:T(8,128)(2,1)S(1)} collective-permute-done((bf16[4,320,864]{2,1,0:T(8,128)(2,1)}, bf16[4,320,864]{2,1,0:T(8,128)(2,1)S(1)}, u32[]{:S(2)}, u32[]{:S(2)}) %collective-permute-start.6) | collective-permute-done | bytes 2211872 | tf_op jit(solution)/shard_map/ppermute | solution.py:94
  282.3 4.0 collective-permute-done.4.refs_1_
  301.8 6.1 %shard_map.151.refs_2_ = bf16[4,4,320,864]{3,2,1,0:T(8,128)(2,1)} custom-call(s32[4]{0:T(128)} %iota_xor_fusion.place, bf16[4,320,864]{2,1,0:T(8,128)(2,1)} %shard_map.150.refs_0_, bf16[4,320,864]{2,1,0:T(8,128)(2,1)} %copy-done.29, bf16[4,320,864]{2,1,0:T(8,128)(2,1)} %collective-permute-done.13.refs_2_), custom_call_target="tpu_custom_call" | custom-call | tf_op jit(solution)/shard_map/pallas_call | solution.py:56
  307.9 6.1 %shard_map.148.refs_2_ = bf16[4,4,320,864]{3,2,1,0:T(8,128)(2,1)} custom-call(s32[4]{0:T(128)} %iota_xor_fusion.place, bf16[4,320,864]{2,1,0:T(8,128)(2,1)} %shard_map.147.refs_0_, bf16[4,320,864]{2,1,0:T(8,128)(2,1)} %copy-done.31, bf16[4,320,864]{2,1,0:T(8,128)(2,1)} %copy-done.30), custom_call_target="tpu_custom_call" | custom-call | tf_op jit(solution)/shard_map/pallas_call | solution.py:56
  321.2 12.3 %collective-permute-done.7.refs_1_ = bf16[2,320,864]{2,1,0:T(8,128)(2,1)} collective-permute-done((bf16[2,320,864]{2,1,0:T(8,128)(2,1)}, bf16[2,320,864]{2,1,0:T(8,128)(2,1)}, u32[]{:S(2)}, u32[]{:S(2)}) %collective-permute-start.7) | collective-permute-done | bytes 1105952 | tf_op jit(solution)/shard_map/ppermute | solution.py:105
  339.3 9.1 %fusion.86 = f32[256,864]{0,1:T(8,128)} fusion(bf16[5120,864]{1,0:T(8,128)(2,1)} %bitcast.158, bf16[256,2560]{1,0:T(8,128)(2,1)} %copy-done.9, bf16[256,2560]{1,0:T(8,128)(2,1)} %copy-done.11), kind=kOutput, calls=%fused_computation.234 | convolution fusion | flops 2270167040 | bytes 12353536 | tf_op jit(solution)/shard_map/dot_general | solution.py:16
  348.4 4.9 fusion.27
  355.6 27.8 %collective-permute-done.22.refs_2_ = bf16[4,320,864]{2,1,0:T(8,128)(2,1)} collective-permute-done((bf16[4,320,864]{2,1,0:T(8,128)(2,1)S(1)}, bf16[4,320,864]{2,1,0:T(8,128)(2,1)}, u32[]{:S(2)}, u32[]{:S(2)}) %collective-permute-start.22) | collective-permute-done | bytes 2211872 | tf_op jit(solution)/shard_map/ppermute | solution.py:94
  390.2 6.1 %shard_map.154.refs_2_ = bf16[4,4,320,864]{3,2,1,0:T(8,128)(2,1)} custom-call(s32[4]{0:T(128)} %iota_xor_fusion.place, bf16[4,320,864]{2,1,0:T(8,128)(2,1)} %shard_map.153.refs_0_, bf16[4,320,864]{2,1,0:T(8,128)(2,1)} %collective-permute-done.20.refs_1_, bf16[4,320,864]{2,1,0:T(8,128)(2,1)} %collective-permute-done.22.refs_2_), custom_call_target="tpu_custom_call" | custom-call | tf_op jit(solution)/shard_map/pallas_call | solution.py:56
  405.8 6.9 %fusion.84 = f32[256,864]{0,1:T(8,128)} fusion(bf16[5120,864]{1,0:T(8,128)(2,1)S(1)} %bitcast.161, bf16[256,2560]{1,0:T(8,128)(2,1)} %copy-done.25, bf16[256,2560]{1,0:T(8,128)(2,1)} %copy-done.27), kind=kOutput, calls=%fused_computation.232 | convolution fusion | flops 2270167040 | bytes 12353536 | tf_op jit(solution)/shard_map/dot_general | solution.py:16
  412.7 3.6 broadcast_select_fusion
  416.4 3.9 fusion.29
  434.2 8.6 %fusion.30 = bf16[256,864]{0,1:T(8,128)(2,1)S(1)} fusion(f32[256,864]{0,1:T(8,128)} %convolution_multiply_fusion.4, bf16[5120,864]{1,0:T(8,128)(2,1)} %bitcast.150, bf16[256,2560]{1,0:T(8,128)(2,1)} %copy-done.21, bf16[256,2560]{1,0:T(8,128)(2,1)} %copy-done.23, f32[256,864]{0,1:T(8,128)} %fusion.84), kind=kOutput, calls=%fused_computation.86 | convolution fusion | flops 2271715328 | bytes 13680640 | tf_op jit(solution)/shard_map/dot_general | solution.py:16
  446.9 7.7 %fusion.28 = bf16[256,864]{0,1:T(8,128)(2,1)S(1)} fusion(f32[256,864]{0,1:T(8,128)} %convolution_multiply_fusion.6, bf16[5120,864]{1,0:T(8,128)(2,1)} %bitcast.151, bf16[256,2560]{1,0:T(8,128)(2,1)S(1)} %copy-done.6, bf16[256,2560]{1,0:T(8,128)(2,1)S(1)} %copy-done.8, f32[256,864]{0,1:T(8,128)} %fusion.86), kind=kOutput, calls=%fused_computation.84 | convolution fusion | flops 2271715328 | bytes 13680640 | tf_op jit(solution)/shard_map/dot_general | solution.py:16
  469.5 4.9 fusion.82
  474.3 7.6 %collective-permute-done.28 = bf16[256,5120]{1,0:T(8,128)(2,1)} collective-permute-done((bf16[256,5120]{1,0:T(8,128)(2,1)}, bf16[256,5120]{1,0:T(8,128)(2,1)}, u32[]{:S(2)}, u32[]{:S(2)}) %collective-permute-start.28) | collective-permute-done | bytes 2621472 | tf_op jit(solution)/shard_map/ppermute | solution.py:134
  484.4 8.9 %fusion.31 = bf16[256,864]{0,1:T(8,128)(2,1)S(1)} fusion(f32[256,864]{0,1:T(8,128)} %convolution_multiply_fusion.3, bf16[5120,864]{1,0:T(8,128)(2,1)} %bitcast.168, f32[256,864]{0,1:T(8,128)} %fusion.82, bf16[256,2560]{1,0:T(8,128)(2,1)S(1)} %get-tuple-element.63, bf16[256,2560]{1,0:T(8,128)(2,1)} %copy-done.19), kind=kOutput, calls=%fused_computation.87 | convolution fusion | flops 2271715328 | bytes 13680640 | tf_op jit(solution)/shard_map/dot_general | solution.py:16
  494.8 5.4 fusion.32
  503.8 4.3 fusion.37
  519.3 4.8 fusion.80
  526.1 7.7 %fusion.33 = bf16[256,864]{0,1:T(8,128)(2,1)S(1)} fusion(f32[256,864]{0,1:T(8,128)S(1)} %convolution_multiply_fusion.1, bf16[5120,864]{1,0:T(8,128)(2,1)} %bitcast.169, f32[256,864]{0,1:T(8,128)} %fusion.80, bf16[256,2560]{1,0:T(8,128)(2,1)S(1)} %get-tuple-element.59, bf16[256,2560]{1,0:T(8,128)(2,1)S(1)} %get-tuple-element.57), kind=kOutput, calls=%fused_computation.89 | convolution fusion | flops 2271715328 | bytes 13680640 | tf_op jit(solution)/shard_map/dot_general | solution.py:16
  536.0 5.2 fusion.34
  544.6 17.2 %all_gather.19 = bf16[8,34,1024]{2,1,0:T(8,128)(2,1)S(1)} all-gather(bf16[1,34,1024]{2,1,0:T(8,128)(2,1)S(1)} %fusion.60), channel_id=1, replica_groups=mesh['o'=4,'i'=4,'mp'=2] {'o','mp'}, dimensions={0}, use_global_device_ids=true | all-gather | bytes 626688 | tf_op jit(solution)/shard_map/all_gather | solution.py:271
  573.1 8.0 %all_to_all.5 = bf16[4,16,1072]{2,1,0:T(8,128)(2,1)S(1)} all-to-all(bf16[4,16,1072]{2,1,0:T(8,128)(2,1)S(1)} %concatenate.80), channel_id=1, replica_groups=mesh['o'=4,'i'=4,'mp'=2] {'i'}, dimensions={0} | all-to-all | bytes 274432 | tf_op jit(solution)/shard_map/all_to_all | solution.py:306
  (371 shorter events, 161.0 us)
Async XLA Ops:
  0.6 232.2 %copy-start = (bf16[16,5120]{1,0:T(8,128)(2,1)S(1)}, bf16[16,5120]{1,0:T(8,128)(2,1)}, u32[]{:S(2)}) copy-start(bf16[16,5120]{1,0:T(8,128)(2,1)} %param.22) | copy-start | bytes 491524
  12.9 171.4 %collective-permute-start.19 = (bf16[256,5120]{1,0:T(8,128)(2,1)}, bf16[256,5120]{1,0:T(8,128)(2,1)}, u32[]{:S(2)}, u32[]{:S(2)}) collective-permute-start(bf16[256,5120]{1,0:T(8,128)(2,1)} %pad_maximum_fusion.8), channel_id=1, source_target_pairs={{8,0},{16,8},{24,16},{9,1},{17,9},{25,17},{10,2},{18,10},{26,18},{... | collective-permute-start | bytes 7864328 | tf_op jit(solution)/shard_map/ppermute | solution.py:134
  14.1 171.7 %collective-permute-start.18 = (bf16[256,5120]{1,0:T(8,128)(2,1)}, bf16[256,5120]{1,0:T(8,128)(2,1)}, u32[]{:S(2)}, u32[]{:S(2)}) collective-permute-start(bf16[256,5120]{1,0:T(8,128)(2,1)} %pad_maximum_fusion.8), channel_id=1, source_target_pairs={{0,8},{8,16},{16,24},{1,9},{9,17},{17,25},{2,10},{10,18},{18,26},{... | collective-permute-start | bytes 7864328 | tf_op jit(solution)/shard_map/ppermute | solution.py:133
  21.1 68.3 %collective-permute-start.3 = (bf16[320,864]{1,0:T(8,128)(2,1)S(1)}, bf16[320,864]{1,0:T(8,128)(2,1)S(1)}, u32[]{:S(2)}, u32[]{:S(2)}) collective-permute-start(bf16[320,864]{1,0:T(8,128)(2,1)S(1)} %copy-done.51), channel_id=1, source_target_pairs={{0,24},{8,0},{16,8},{24,16},{1,25},{9,1},{17,9},{25,17},{2,26},{10... | collective-permute-start | bytes 1658888 | tf_op jit(solution)/shard_map/ppermute | solution.py:75
  25.4 76.2 %collective-permute-start.10 = (bf16[320,864]{1,0:T(8,128)(2,1)S(1)}, bf16[320,864]{1,0:T(8,128)(2,1)}, u32[]{:S(2)}, u32[]{:S(2)}) collective-permute-start(bf16[320,864]{1,0:T(8,128)(2,1)S(1)} %get-tuple-element.72), channel_id=1, source_target_pairs={{0,24},{8,0},{16,8},{24,16},{1,25},{9,1},{17,9},{25,17},{2,26},{10... | collective-permute-start | bytes 1658888 | tf_op jit(solution)/shard_map/ppermute | solution.py:75
  28.1 161.7 %collective-permute-start = (bf16[256,5120]{1,0:T(8,128)(2,1)}, bf16[256,5120]{1,0:T(8,128)(2,1)}, u32[]{:S(2)}, u32[]{:S(2)}) collective-permute-start(bf16[256,5120]{1,0:T(8,128)(2,1)} %pad_maximum_fusion.8), channel_id=1, source_target_pairs={{0,1},{1,0},{2,3},{3,2},{4,5},{5,4},{6,7},{7,6},{8,9},{9,8},{10,11... | collective-permute-start | bytes 7864328 | tf_op jit(solution)/shard_map/ppermute | solution.py:157
  89.4 25.7 %collective-permute-start.8 = (bf16[320,864]{1,0:T(8,128)(2,1)}, bf16[320,864]{1,0:T(8,128)(2,1)}, u32[]{:S(2)}, u32[]{:S(2)}) collective-permute-start(bf16[320,864]{1,0:T(8,128)(2,1)} %get-tuple-element.73), channel_id=1, source_target_pairs={{0,8},{8,16},{16,24},{24,0},{1,9},{9,17},{17,25},{25,1},{2,10},{10... | collective-permute-start | bytes 1658888 | tf_op jit(solution)/shard_map/ppermute | solution.py:75
  101.6 61.7 %collective-permute-start.9 = (bf16[320,864]{1,0:T(8,128)(2,1)}, bf16[320,864]{1,0:T(8,128)(2,1)}, u32[]{:S(2)}, u32[]{:S(2)}) collective-permute-start(bf16[320,864]{1,0:T(8,128)(2,1)} %get-tuple-element.75), channel_id=1, source_target_pairs={{0,16},{8,24},{16,0},{24,8},{1,17},{9,25},{17,1},{25,9},{2,18},{10... | collective-permute-start | bytes 1658888 | tf_op jit(solution)/shard_map/ppermute | solution.py:75
  115.1 60.8 %collective-permute-start.1 = (bf16[320,864]{1,0:T(8,128)(2,1)}, bf16[320,864]{1,0:T(8,128)(2,1)}, u32[]{:S(2)}, u32[]{:S(2)}) collective-permute-start(bf16[320,864]{1,0:T(8,128)(2,1)} %get-tuple-element.81), channel_id=1, source_target_pairs={{0,8},{8,16},{16,24},{24,0},{1,9},{9,17},{17,25},{25,1},{2,10},{10... | collective-permute-start | bytes 1658888 | tf_op jit(solution)/shard_map/ppermute | solution.py:75
  163.4 16.2 %collective-permute-start.2 = (bf16[320,864]{1,0:T(8,128)(2,1)}, bf16[320,864]{1,0:T(8,128)(2,1)}, u32[]{:S(2)}, u32[]{:S(2)}) collective-permute-start(bf16[320,864]{1,0:T(8,128)(2,1)} %get-tuple-element.83), channel_id=1, source_target_pairs={{0,16},{8,24},{16,0},{24,8},{1,17},{9,25},{17,1},{25,9},{2,18},{10... | collective-permute-start | bytes 1658888 | tf_op jit(solution)/shard_map/ppermute | solution.py:75
  175.9 112.2 %collective-permute-start.17 = (bf16[320,864]{1,0:T(8,128)(2,1)}, bf16[320,864]{1,0:T(8,128)(2,1)S(1)}, u32[]{:S(2)}, u32[]{:S(2)}) collective-permute-start(bf16[320,864]{1,0:T(8,128)(2,1)} %get-tuple-element.76), channel_id=1, source_target_pairs={{0,24},{8,0},{16,8},{24,16},{1,25},{9,1},{17,9},{25,17},{2,26},{10... | collective-permute-start | bytes 1658888 | tf_op jit(solution)/shard_map/ppermute | solution.py:75
  179.5 53.0 %collective-permute-start.13 = (bf16[4,320,864]{2,1,0:T(8,128)(2,1)}, bf16[4,320,864]{2,1,0:T(8,128)(2,1)}, u32[]{:S(2)}, u32[]{:S(2)}) collective-permute-start(bf16[4,320,864]{2,1,0:T(8,128)(2,1)} %shard_map.150.refs_0_), channel_id=1, source_target_pairs={{0,4},{2,6},{4,0},{6,2},{1,5},{3,7},{5,1},{7,3},{8,12},{10,14},{12... | collective-permute-start | bytes 6635528 | tf_op jit(solution)/shard_map/ppermute | solution.py:94
  184.2 53.0 %collective-permute-start.11 = (bf16[4,320,864]{2,1,0:T(8,128)(2,1)}, bf16[4,320,864]{2,1,0:T(8,128)(2,1)S(1)}, u32[]{:S(2)}, u32[]{:S(2)}) collective-permute-start(bf16[4,320,864]{2,1,0:T(8,128)(2,1)} %shard_map.150.refs_0_), channel_id=1, source_target_pairs={{0,2},{2,0},{4,6},{6,4},{1,3},{3,1},{5,7},{7,5},{8,10},{10,8},{12,... | collective-permute-start | bytes 6635528 | tf_op jit(solution)/shard_map/ppermute | solution.py:94
  185.8 94.0 %collective-permute-start.6 = (bf16[4,320,864]{2,1,0:T(8,128)(2,1)}, bf16[4,320,864]{2,1,0:T(8,128)(2,1)S(1)}, u32[]{:S(2)}, u32[]{:S(2)}) collective-permute-start(bf16[4,320,864]{2,1,0:T(8,128)(2,1)} %shard_map.147.refs_0_), channel_id=1, source_target_pairs={{0,4},{2,6},{4,0},{6,2},{1,5},{3,7},{5,1},{7,3},{8,12},{10,14},{12... | collective-permute-start | bytes 6635528 | tf_op jit(solution)/shard_map/ppermute | solution.py:94
  189.8 96.6 %collective-permute-start.4 = (bf16[4,320,864]{2,1,0:T(8,128)(2,1)S(1)}, bf16[4,320,864]{2,1,0:T(8,128)(2,1)S(1)}, u32[]{:S(2)}, u32[]{:S(2)}) collective-permute-start(bf16[4,320,864]{2,1,0:T(8,128)(2,1)S(1)} %copy-done.2), channel_id=1, source_target_pairs={{0,2},{2,0},{4,6},{6,4},{1,3},{3,1},{5,7},{7,5},{8,10},{10,8},{12,... | collective-permute-start | bytes 6635528 | tf_op jit(solution)/shard_map/ppermute | solution.py:94
  232.6 57.1 %collective-permute-start.15 = (bf16[320,864]{1,0:T(8,128)(2,1)S(1)}, bf16[320,864]{1,0:T(8,128)(2,1)S(1)}, u32[]{:S(2)}, u32[]{:S(2)}) collective-permute-start(bf16[320,864]{1,0:T(8,128)(2,1)S(1)} %copy-done.50), channel_id=1, source_target_pairs={{0,8},{8,16},{16,24},{24,0},{1,9},{9,17},{17,25},{25,1},{2,10},{10... | collective-permute-start | bytes 1658888 | tf_op jit(solution)/shard_map/ppermute | solution.py:75
  237.2 58.1 %collective-permute-start.16 = (bf16[320,864]{1,0:T(8,128)(2,1)S(1)}, bf16[320,864]{1,0:T(8,128)(2,1)S(1)}, u32[]{:S(2)}, u32[]{:S(2)}) collective-permute-start(bf16[320,864]{1,0:T(8,128)(2,1)S(1)} %copy-done.49), channel_id=1, source_target_pairs={{0,16},{8,24},{16,0},{24,8},{1,17},{9,25},{17,1},{25,9},{2,18},{10... | collective-permute-start | bytes 1658888 | tf_op jit(solution)/shard_map/ppermute | solution.py:75
  279.7 34.3 %collective-permute-start.14 = (bf16[2,320,864]{2,1,0:T(8,128)(2,1)}, bf16[2,320,864]{2,1,0:T(8,128)(2,1)}, u32[]{:S(2)}, u32[]{:S(2)}) collective-permute-start(bf16[2,320,864]{2,1,0:T(8,128)(2,1)} %slice.187), channel_id=1, source_target_pairs={{0,2},{2,0},{4,6},{6,4},{1,3},{3,1},{5,7},{7,5},{8,10},{10,8},{12,... | collective-permute-start | bytes 3317768 | tf_op jit(solution)/shard_map/ppermute | solution.py:105
  286.4 29.1 %collective-permute-start.12 = (bf16[2,320,864]{2,1,0:T(8,128)(2,1)}, bf16[2,320,864]{2,1,0:T(8,128)(2,1)}, u32[]{:S(2)}, u32[]{:S(2)}) collective-permute-start(bf16[2,320,864]{2,1,0:T(8,128)(2,1)} %slice.186), channel_id=1, source_target_pairs={{0,4},{2,6},{4,0},{6,2},{1,5},{3,7},{5,1},{7,3},{8,12},{10,14},{12... | collective-permute-start | bytes 3317768 | tf_op jit(solution)/shard_map/ppermute | solution.py:105
  288.1 45.4 %collective-permute-start.7 = (bf16[2,320,864]{2,1,0:T(8,128)(2,1)}, bf16[2,320,864]{2,1,0:T(8,128)(2,1)}, u32[]{:S(2)}, u32[]{:S(2)}) collective-permute-start(bf16[2,320,864]{2,1,0:T(8,128)(2,1)} %slice.185), channel_id=1, source_target_pairs={{0,2},{2,0},{4,6},{6,4},{1,3},{3,1},{5,7},{7,5},{8,10},{10,8},{12,... | collective-permute-start | bytes 3317768 | tf_op jit(solution)/shard_map/ppermute | solution.py:105
  289.7 44.7 %collective-permute-start.5 = (bf16[2,320,864]{2,1,0:T(8,128)(2,1)}, bf16[2,320,864]{2,1,0:T(8,128)(2,1)}, u32[]{:S(2)}, u32[]{:S(2)}) collective-permute-start(bf16[2,320,864]{2,1,0:T(8,128)(2,1)} %slice.184), channel_id=1, source_target_pairs={{0,4},{2,6},{4,0},{6,2},{1,5},{3,7},{5,1},{7,3},{8,12},{10,14},{12... | collective-permute-start | bytes 3317768 | tf_op jit(solution)/shard_map/ppermute | solution.py:105
  295.4 100.9 %collective-permute-start.24 = (bf16[256,5120]{1,0:T(8,128)(2,1)}, bf16[256,5120]{1,0:T(8,128)(2,1)}, u32[]{:S(2)}, u32[]{:S(2)}) collective-permute-start(bf16[256,5120]{1,0:T(8,128)(2,1)} %broadcast_select_fusion.1), channel_id=1, source_target_pairs={{0,1},{1,0},{2,3},{3,2},{4,5},{5,4},{6,7},{7,6},{8,9},{9,8},{10,11... | collective-permute-start | bytes 7864328 | tf_op jit(solution)/shard_map/ppermute | solution.py:157
  314.0 98.7 %collective-permute-start.25 = (bf16[256,5120]{1,0:T(8,128)(2,1)}, bf16[256,5120]{1,0:T(8,128)(2,1)}, u32[]{:S(2)}, u32[]{:S(2)}) collective-permute-start(bf16[256,5120]{1,0:T(8,128)(2,1)} %collective-permute-done.19), channel_id=1, source_target_pairs={{8,0},{16,8},{9,1},{17,9},{10,2},{18,10},{11,3},{19,11},{12,4},{20... | collective-permute-start | bytes 7864328 | tf_op jit(solution)/shard_map/ppermute | solution.py:134
  315.5 97.2 %collective-permute-start.26 = (bf16[256,5120]{1,0:T(8,128)(2,1)}, bf16[256,5120]{1,0:T(8,128)(2,1)}, u32[]{:S(2)}, u32[]{:S(2)}) collective-permute-start(bf16[256,5120]{1,0:T(8,128)(2,1)} %collective-permute-done.18), channel_id=1, source_target_pairs={{8,16},{16,24},{9,17},{17,25},{10,18},{18,26},{11,19},{19,27},{12,... | collective-permute-start | bytes 7864328 | tf_op jit(solution)/shard_map/ppermute | solution.py:133
  333.5 49.9 %collective-permute-start.22 = (bf16[4,320,864]{2,1,0:T(8,128)(2,1)S(1)}, bf16[4,320,864]{2,1,0:T(8,128)(2,1)}, u32[]{:S(2)}, u32[]{:S(2)}) collective-permute-start(bf16[4,320,864]{2,1,0:T(8,128)(2,1)S(1)} %copy-done.3), channel_id=1, source_target_pairs={{0,4},{2,6},{4,0},{6,2},{1,5},{3,7},{5,1},{7,3},{8,12},{10,14},{12... | collective-permute-start | bytes 6635528 | tf_op jit(solution)/shard_map/ppermute | solution.py:94
  334.4 52.9 %collective-permute-start.20 = (bf16[4,320,864]{2,1,0:T(8,128)(2,1)S(1)}, bf16[4,320,864]{2,1,0:T(8,128)(2,1)}, u32[]{:S(2)}, u32[]{:S(2)}) collective-permute-start(bf16[4,320,864]{2,1,0:T(8,128)(2,1)S(1)} %copy-done.3), channel_id=1, source_target_pairs={{0,2},{2,0},{4,6},{6,4},{1,3},{3,1},{5,7},{7,5},{8,10},{10,8},{12,... | collective-permute-start | bytes 6635528 | tf_op jit(solution)/shard_map/ppermute | solution.py:94
  385.8 44.9 %collective-permute-start.23 = (bf16[2,320,864]{2,1,0:T(8,128)(2,1)}, bf16[2,320,864]{2,1,0:T(8,128)(2,1)}, u32[]{:S(2)}, u32[]{:S(2)}) collective-permute-start(bf16[2,320,864]{2,1,0:T(8,128)(2,1)} %slice.191), channel_id=1, source_target_pairs={{0,2},{2,0},{4,6},{6,4},{1,3},{3,1},{5,7},{7,5},{8,10},{10,8},{12,... | collective-permute-start | bytes 3317768 | tf_op jit(solution)/shard_map/ppermute | solution.py:105
  389.7 41.0 %collective-permute-start.21 = (bf16[2,320,864]{2,1,0:T(8,128)(2,1)}, bf16[2,320,864]{2,1,0:T(8,128)(2,1)}, u32[]{:S(2)}, u32[]{:S(2)}) collective-permute-start(bf16[2,320,864]{2,1,0:T(8,128)(2,1)} %slice.190), channel_id=1, source_target_pairs={{0,4},{2,6},{4,0},{6,2},{1,5},{3,7},{5,1},{7,3},{8,12},{10,14},{12... | collective-permute-start | bytes 3317768 | tf_op jit(solution)/shard_map/ppermute | solution.py:105
  416.3 44.4 %collective-permute-start.27 = (bf16[256,5120]{1,0:T(8,128)(2,1)}, bf16[256,5120]{1,0:T(8,128)(2,1)}, u32[]{:S(2)}, u32[]{:S(2)}) collective-permute-start(bf16[256,5120]{1,0:T(8,128)(2,1)} %broadcast_select_fusion), channel_id=1, source_target_pairs={{0,1},{1,0},{2,3},{3,2},{4,5},{5,4},{6,7},{7,6},{8,9},{9,8},{10,11... | collective-permute-start | bytes 7864328 | tf_op jit(solution)/shard_map/ppermute | solution.py:157
  420.3 61.6 %collective-permute-start.28 = (bf16[256,5120]{1,0:T(8,128)(2,1)}, bf16[256,5120]{1,0:T(8,128)(2,1)}, u32[]{:S(2)}, u32[]{:S(2)}) collective-permute-start(bf16[256,5120]{1,0:T(8,128)(2,1)} %collective-permute-done.25), channel_id=1, source_target_pairs={{8,0},{9,1},{10,2},{11,3},{12,4},{13,5},{14,6},{15,7}} | collective-permute-start | bytes 7864328 | tf_op jit(solution)/shard_map/ppermute | solution.py:134
  421.7 60.2 %collective-permute-start.29 = (bf16[256,5120]{1,0:T(8,128)(2,1)}, bf16[256,5120]{1,0:T(8,128)(2,1)}, u32[]{:S(2)}, u32[]{:S(2)}) collective-permute-start(bf16[256,5120]{1,0:T(8,128)(2,1)} %collective-permute-done.26), channel_id=1, source_target_pairs={{16,24},{17,25},{18,26},{19,27},{20,28},{21,29},{22,30},{23,31}} | collective-permute-start | bytes 7864328 | tf_op jit(solution)/shard_map/ppermute | solution.py:133
  484.3 27.7 %collective-permute-start.30 = (bf16[256,5120]{1,0:T(8,128)(2,1)S(1)}, bf16[256,5120]{1,0:T(8,128)(2,1)}, u32[]{:S(2)}, u32[]{:S(2)}) collective-permute-start(bf16[256,5120]{1,0:T(8,128)(2,1)S(1)} %select_select_fusion), channel_id=1, source_target_pairs={{0,1},{1,0},{2,3},{3,2},{4,5},{5,4},{6,7},{7,6},{8,9},{9,8},{10,11... | collective-permute-start | bytes 7864328 | tf_op jit(solution)/shard_map/ppermute | solution.py:157
  (88 other events, 1142.0 us)
where the time goes:
time: 593 us; the launch traced here: 583 us
  waiting for transfers between devices  267 us (45%)
  matrix products  126 us (21%)
  local copies, waits for them, and re-layouts  38.2 us (6%)
  starting transfers between devices  38.1 us (6%)
  Pallas kernels  38 us (6%)
  other arithmetic  33.8 us (6%)
  blocking collectives  27.8 us (5%)
  between operations  13.8 us (2%)
    ppermute x9, waiting for transfers between devices, exchange(): lax.ppermute(pieces[d], 'o', [(s, (s + d) % r) for s in range(r)])  135 us
    ppermute x6, waiting for transfers between devices, neighbours(): lax.ppermute(part, 'i', [(s, s ^ bit) for s in range(p)])  112 us
    dot_general x22, matrix products, matmul(): return jnp.dot(left, right, preferred_element_type=jnp.float32)  91 us
    pallas_call x9, Pallas kernels, copied(): pl.pallas_call(kernel, out_shape=jax.ShapeDtypeStruct(shape, arrays[0].dt...  38 us
    dot_general x32, matrix products, contract(): lax.dot_general(left, right, (((left_dim,), (right_dim,)), ((), ())), pre...  33.7 us
    all_gather x1, blocking collectives, per_device(): lax.all_gather(sums, ('o', 'mp'), axis=0).astype(f32)  17.2 us
    ppermute x6, waiting for transfers between devices, assembled(): lax.ppermute(piece, 'i', [(s, s ^ bit) for s in range(p)])  12.6 us
  transfers between devices with their start and end apart: 31, of which 13 were waited for; matrix products, arithmetic and copies ran while one was open for 24% of the time, Pallas kernels for 7%

commit v1 on v0

--- a/solution.py
+++ b/solution.py
@@ -61,6 +61,35 @@
         scratch_shapes=[pltpu.VMEM(a.shape, a.dtype) for a in arrays]
         + [pltpu.SemaphoreType.DMA((count,)), pltpu.SemaphoreType.DMA((count,))],
         input_output_aliases={} if into is None else {1 + count: 0},
+        compiler_params=pltpu.CompilerParams(
+            vmem_limit_bytes=(1 << 20) + 2 * sum(a.size * a.dtype.itemsize for a in arrays)
+        ),
+    )(places, *arrays, *extra)
+
+
+def gathered(shape, places, arrays, plan, into=None):
+    count = len(arrays)
+
+    def kernel(place, *refs):
+        copies = [
+            pltpu.make_async_copy(source, to, refs[-1].at[k])
+            for k, (source, to) in enumerate(zip(refs[:count], plan(place, refs[-2])))
+        ]
+        for copy in copies:
+            copy.start()
+        for copy in copies:
+            copy.wait()
+
+    anywhere, on_chip = pl.BlockSpec(memory_space=pl.ANY), pl.BlockSpec(memory_space=pltpu.VMEM)
+    extra = [] if into is None else [into]
+    return pl.pallas_call(
+        kernel,
+        out_shape=pltpu.VMEM(shape, arrays[0].dtype),
+        in_specs=[pl.BlockSpec(memory_space=pltpu.SMEM)] + [anywhere] * count + [on_chip] * len(extra),
+        out_specs=on_chip,
+        scratch_shapes=[pltpu.SemaphoreType.DMA((count,))],
+        input_output_aliases={} if into is None else {1 + count: 0},
+        compiler_params=pltpu.CompilerParams(vmem_limit_bytes=1 << 20),
     )(places, *arrays, *extra)
 
 
@@ -104,13 +133,13 @@
     corner = [
         lax.ppermute(piece, "i", [(s, s ^ bit) for s in range(p)]) for piece, bit in zip(passed, (2, 1))
     ]
-    out = copied(
+    out = gathered(
         shape,
         places,
         [part] + near,
         lambda place, target: [target.at[:, place[k]] for k in range(3)],
     )
-    out = copied(
+    out = gathered(
         shape,
         places,
         corner,
@@ -155,12 +184,30 @@
         whole = lambda a: a.swapaxes(0, 1).reshape(block.shape[0], -1)
         return whole(both[:, :, :width]), whole(both[:, :, width:])
     other = lax.ppermute(block, "mp", [(0, 1), (1, 0)])
-    first = lax.axis_index("mp") == 0
-    south, north = jnp.where(first, block, other), jnp.where(first, other, block)
-    return (
-        jnp.concatenate([south[:, :width], north[:, :width]], axis=1),
-        jnp.concatenate([south[:, width:], north[:, width:]], axis=1),
-    )
+    c = lax.axis_index("mp")
+
+    def kernel(place, own, received, normed, gradient, sems):
+        copies = []
+        for k, (source, at) in enumerate(((own, place[0]), (received, place[1]))):
+            columns = pl.ds(pl.multiple_of(at * width, 128), width)
+            for j, target in enumerate((normed, gradient)):
+                part = source.at[:, j * width : (j + 1) * width]
+                copies.append(pltpu.make_async_copy(part, target.at[:, columns], sems.at[2 * k + j]))
+        for copy in copies:
+            copy.start()
+        for copy in copies:
+            copy.wait()
+
+    anywhere, on_chip = pl.BlockSpec(memory_space=pl.ANY), pl.BlockSpec(memory_space=pltpu.VMEM)
+    shape = (block.shape[0], 2 * width)
+    return pl.pallas_call(
+        kernel,
+        out_shape=[pltpu.VMEM(shape, block.dtype)] * 2,
+        in_specs=[pl.BlockSpec(memory_space=pltpu.SMEM), anywhere, anywhere],
+        out_specs=[on_chip] * 2,
+        scratch_shapes=[pltpu.SemaphoreType.DMA((4,))],
+        compiler_params=pltpu.CompilerParams(vmem_limit_bytes=1 << 20),
+    )(jnp.stack([c, 1 - c]).astype(jnp.int32), block, other)
 
 
 def per_device(

time: 593 us -> 595 us (level)
  waiting for transfers between devices: 267 us -> 289 us
  other arithmetic: 33.8 us -> 14.2 us
  Pallas kernels: 38 us -> 26.6 us
  matrix products: 126 us -> 132 us
    pallas_call x9 -> x3, Pallas kernels: 38 us -> 5.63 us  [copied(): pl.pallas_call(kernel, out_shape=jax.ShapeDtypeStruct(shape, arrays[0].dt...]
    pallas_call x0 -> x10, Pallas kernels: none -> 20.9 us  [the longest x4 11.1 us: across(): pl.pallas_call(kernel, out_shape=[pltpu.VMEM(shape, block.dtype)] * 2, in...]
    select_n x4 -> x0, other arithmetic: 10.3 us -> none  [across(): jnp.where(first, other, block)]
    ppermute x3, waiting for transfers between devices: 7.57 us -> 15.6 us  [gather_path(): lax.ppermute(down[-1], 'o', [(s, s - 1) for s in range(1, r - k + 1)])]
    dynamic_slice x0 -> x8, local copies, waits for them, and re-layouts: none -> 7.67 us  [per_device(): share = lambda t: lax.dynamic_slice(t, (0, o * p * block), (seq, p * block))]
    ppermute x6, waiting for transfers between devices: 12.6 us -> 20.3 us  [assembled(): lax.ppermute(piece, 'i', [(s, s ^ bit) for s in range(p)])]
    dot_general x22, matrix products: 91 us -> 97.7 us  [matmul(): return jnp.dot(left, right, preferred_element_type=jnp.float32)]
    concatenate x4 -> x0, other arithmetic: 6.45 us -> none  [across(): jnp.concatenate([south[:, width:], north[:, width:]], axis=1)]
  transfers between devices with their start and end apart: 31 -> 31, of which waited for: 13 -> 14; matrix products, arithmetic and copies ran while one was open for 24% -> 22% of each run, Pallas kernels for 7% -> 4%
where the time goes in v1:
time: 595 us; the launch traced here: 584 us
  waiting for transfers between devices  289 us (49%)
  matrix products  132 us (22%)
  local copies, waits for them, and re-layouts  42 us (7%)
  starting transfers between devices  41.6 us (7%)
  Pallas kernels  26.6 us (4%)
  blocking collectives  26 us (4%)
  other arithmetic  14.2 us (2%)
  between operations  13.2 us (2%)
    ppermute x9, waiting for transfers between devices, exchange(): lax.ppermute(pieces[d], 'o', [(s, (s + d) % r) for s in range(r)])  141 us
    ppermute x6, waiting for transfers between devices, neighbours(): lax.ppermute(part, 'i', [(s, s ^ bit) for s in range(p)])  111 us
    dot_general x22, matrix products, matmul(): return jnp.dot(left, right, preferred_element_type=jnp.float32)  97.7 us
    dot_general x32, matrix products, contract(): lax.dot_general(left, right, (((left_dim,), (right_dim,)), ((), ())), pre...  32.9 us
    ppermute x6, waiting for transfers between devices, assembled(): lax.ppermute(piece, 'i', [(s, s ^ bit) for s in range(p)])  20.3 us
    ppermute x3, waiting for transfers between devices, gather_path(): lax.ppermute(down[-1], 'o', [(s, s - 1) for s in range(1, r - k + 1)])  15.6 us
    all_gather x1, blocking collectives, per_device(): lax.all_gather(sums, ('o', 'mp'), axis=0).astype(f32)  15.5 us
  transfers between devices with their start and end apart: 31, of which 14 were waited for; matrix products, arithmetic and copies ran while one was open for 22% of the time, Pallas kernels for 4%

profile of v1, /device:TPU:0, one launch (start us, length us, event | category | flops | bytes accessed | tf_op | source)
XLA Modules:
  0.0 584.1 jit_solution(9332458718924467505)
XLA Ops:
  1.5 4.2 constant_dynamic-slice_fusion.22
  11.6 6.8 %collective-permute-start.18 = (bf16[256,5120]{1,0:T(8,128)(2,1)S(1)}, bf16[256,5120]{1,0:T(8,128)(2,1)}, u32[]{:S(2)}, u32[]{:S(2)}) collective-permute-start(bf16[256,5120]{1,0:T(8,128)(2,1)S(1)} %pad_maximum_fusion.own), channel_id=1, source_target_pairs={{0,8},{8,16},{16,24},{1,9},{9,17},{17,25},{2,10},{10,18},{18,26},{... | collective-permute-start | bytes 7864328 | tf_op jit(solution)/shard_map/ppermute | solution.py:162
  25.1 61.3 %collective-permute-done.3.refs_3_ = bf16[320,864]{1,0:T(8,128)(2,1)S(1)} collective-permute-done((bf16[320,864]{1,0:T(8,128)(2,1)S(1)}, bf16[320,864]{1,0:T(8,128)(2,1)S(1)}, u32[]{:S(2)}, u32[]{:S(2)}) %collective-permute-start.3) | collective-permute-done | bytes 552992 | tf_op jit(solution)/shard_map/ppermute | solution.py:104
  87.7 11.0 %collective-permute-done.10.refs_3_ = bf16[320,864]{1,0:T(8,128)(2,1)S(1)} collective-permute-done((bf16[320,864]{1,0:T(8,128)(2,1)S(1)}, bf16[320,864]{1,0:T(8,128)(2,1)S(1)}, u32[]{:S(2)}, u32[]{:S(2)}) %collective-permute-start.10) | collective-permute-done | bytes 552992 | tf_op jit(solution)/shard_map/ppermute | solution.py:104
  101.1 11.0 %collective-permute-done.8.refs_1_ = bf16[320,864]{1,0:T(8,128)(2,1)S(1)} collective-permute-done((bf16[320,864]{1,0:T(8,128)(2,1)S(1)}, bf16[320,864]{1,0:T(8,128)(2,1)S(1)}, u32[]{:S(2)}, u32[]{:S(2)}) %collective-permute-start.8) | collective-permute-done | bytes 552992 | tf_op jit(solution)/shard_map/ppermute | solution.py:104
  115.0 45.6 %collective-permute-done.9.refs_2_ = bf16[320,864]{1,0:T(8,128)(2,1)} collective-permute-done((bf16[320,864]{1,0:T(8,128)(2,1)}, bf16[320,864]{1,0:T(8,128)(2,1)}, u32[]{:S(2)}, u32[]{:S(2)}) %collective-permute-start.9) | collective-permute-done | bytes 552992 | tf_op jit(solution)/shard_map/ppermute | solution.py:104
  171.8 4.9 collective-permute-done.2.refs_2_
  185.9 3.9 broadcast_select_fusion.1.own
  190.6 31.1 %collective-permute-done.13.refs_2_ = bf16[4,320,864]{2,1,0:T(8,128)(2,1)S(1)} collective-permute-done((bf16[4,320,864]{2,1,0:T(8,128)(2,1)S(1)}, bf16[4,320,864]{2,1,0:T(8,128)(2,1)S(1)}, u32[]{:S(2)}, u32[]{:S(2)}) %collective-permute-start.13) | collective-permute-done | bytes 2211872 | tf_op jit(solution)/shard_map/ppermute | solution.py:123
  223.5 5.9 %collective-permute-done.11.refs_1_ = bf16[4,320,864]{2,1,0:T(8,128)(2,1)S(1)} collective-permute-done((bf16[4,320,864]{2,1,0:T(8,128)(2,1)S(1)}, bf16[4,320,864]{2,1,0:T(8,128)(2,1)S(1)}, u32[]{:S(2)}, u32[]{:S(2)}) %collective-permute-start.11) | collective-permute-done | bytes 2211872 | tf_op jit(solution)/shard_map/ppermute | solution.py:123
  232.0 37.9 %collective-permute-done.6.refs_2_ = bf16[4,320,864]{2,1,0:T(8,128)(2,1)S(1)} collective-permute-done((bf16[4,320,864]{2,1,0:T(8,128)(2,1)S(1)}, bf16[4,320,864]{2,1,0:T(8,128)(2,1)S(1)}, u32[]{:S(2)}, u32[]{:S(2)}) %collective-permute-start.6) | collective-permute-done | bytes 2211872 | tf_op jit(solution)/shard_map/ppermute | solution.py:123
  271.5 7.1 %collective-permute-done.4.refs_1_ = bf16[4,320,864]{2,1,0:T(8,128)(2,1)S(1)} collective-permute-done((bf16[4,320,864]{2,1,0:T(8,128)(2,1)S(1)}, bf16[4,320,864]{2,1,0:T(8,128)(2,1)S(1)}, u32[]{:S(2)}, u32[]{:S(2)}) %collective-permute-start.4) | collective-permute-done | bytes 2211872 | tf_op jit(solution)/shard_map/ppermute | solution.py:123
  288.0 7.7 %collective-permute-done.16.refs_2_ = bf16[320,864]{1,0:T(8,128)(2,1)S(1)} collective-permute-done((bf16[320,864]{1,0:T(8,128)(2,1)S(1)}, bf16[320,864]{1,0:T(8,128)(2,1)S(1)}, u32[]{:S(2)}, u32[]{:S(2)}) %collective-permute-start.16) | collective-permute-done | bytes 552992 | tf_op jit(solution)/shard_map/ppermute | solution.py:104
  307.7 18.2 %collective-permute-done.7.refs_1_ = bf16[2,320,864]{2,1,0:T(8,128)(2,1)S(1)} collective-permute-done((bf16[2,320,864]{2,1,0:T(8,128)(2,1)S(1)}, bf16[2,320,864]{2,1,0:T(8,128)(2,1)S(1)}, u32[]{:S(2)}, u32[]{:S(2)}) %collective-permute-start.7) | collective-permute-done | bytes 1105952 | tf_op jit(solution)/shard_map/ppermute | solution.py:134
  329.8 8.4 %fusion.58 = f32[256,864]{0,1:T(8,128)} fusion(bf16[256,5120]{1,0:T(8,128)(2,1)} %copy-done.6, bf16[5120,864]{1,0:T(8,128)(2,1)S(1)} %bitcast.196), kind=kOutput, calls=%fused_computation.183 | convolution fusion | flops 2264924160 | bytes 12353536 | tf_op jit(solution)/shard_map/dot_general | solution.py:16
  338.2 6.0 %fusion.27 = bf16[256,864]{0,1:T(8,128)(2,1)S(1)} fusion(f32[256,864]{0,1:T(8,128)} %convolution_multiply_fusion.7, bf16[256,5120]{1,0:T(8,128)(2,1)} %copy-done.6, bf16[5120,864]{1,0:T(8,128)(2,1)S(1)} %bitcast.202, f32[256,864]{0,1:T(8,128)} %fusion.58), kind=kOutput, calls=%fused_computation.51 | convolution fusion | flops 2266472448 | bytes 13680640 | tf_op jit(solution)/shard_map/dot_general | solution.py:16
  346.7 29.5 %collective-permute-done.22.refs_2_ = bf16[4,320,864]{2,1,0:T(8,128)(2,1)} collective-permute-done((bf16[4,320,864]{2,1,0:T(8,128)(2,1)S(1)}, bf16[4,320,864]{2,1,0:T(8,128)(2,1)}, u32[]{:S(2)}, u32[]{:S(2)}) %collective-permute-start.22) | collective-permute-done | bytes 2211872 | tf_op jit(solution)/shard_map/ppermute | solution.py:123
  383.9 3.6 shard_map.155.refs_2_
  387.6 3.1 shard_map.157
  393.5 7.3 %fusion.59 = f32[256,864]{0,1:T(8,128)S(1)} fusion(bf16[256,5120]{1,0:T(8,128)(2,1)S(1)} %get-tuple-element.42, bf16[5120,864]{1,0:T(8,128)(2,1)} %bitcast.197), kind=kOutput, calls=%fused_computation.184 | convolution fusion | flops 2264924160 | bytes 12353536 | tf_op jit(solution)/shard_map/dot_general | solution.py:16
  400.9 7.7 %fusion.29 = bf16[256,864]{0,1:T(8,128)(2,1)S(1)} fusion(f32[256,864]{0,1:T(8,128)S(1)} %convolution_multiply_fusion.5, bf16[256,5120]{1,0:T(8,128)(2,1)S(1)} %get-tuple-element.42, bf16[5120,864]{1,0:T(8,128)(2,1)} %bitcast.203, f32[256,864]{0,1:T(8,128)S(1)} %fusion.59), kind=kOutput, calls=%fused_computation.53 | convolution fusion | flops 2266472448 | bytes 13680640 | tf_op jit(solution)/shard_map/dot_general | solution.py:16
  423.9 8.5 %fusion.30 = bf16[256,864]{0,1:T(8,128)(2,1)S(1)} fusion(f32[256,864]{0,1:T(8,128)S(1)} %convolution_multiply_fusion.4, bf16[256,5120]{1,0:T(8,128)(2,1)} %copy-done.11, bf16[5120,864]{1,0:T(8,128)(2,1)S(1)} %bitcast.188, f32[256,864]{0,1:T(8,128)} %copy-done.49), kind=kOutput, calls=%fused_computation.54 | convolution fusion | flops 2266472448 | bytes 13680640 | tf_op jit(solution)/shard_map/dot_general | solution.py:16
  433.9 5.0 fusion.28
  451.5 8.3 %fusion.60 = f32[256,864]{0,1:T(8,128)} fusion(bf16[256,5120]{1,0:T(8,128)(2,1)S(1)} %get-tuple-element.46, bf16[5120,864]{1,0:T(8,128)(2,1)} %bitcast.198), kind=kOutput, calls=%fused_computation.185 | convolution fusion | flops 2264924160 | bytes 12353536 | tf_op jit(solution)/shard_map/dot_general | solution.py:16
  459.8 15.6 %collective-permute-done.28 = bf16[256,5120]{1,0:T(8,128)(2,1)} collective-permute-done((bf16[256,5120]{1,0:T(8,128)(2,1)}, bf16[256,5120]{1,0:T(8,128)(2,1)}, u32[]{:S(2)}, u32[]{:S(2)}) %collective-permute-start.28) | collective-permute-done | bytes 2621472 | tf_op jit(solution)/shard_map/ppermute | solution.py:163
  477.9 8.3 %fusion.31 = bf16[256,864]{0,1:T(8,128)(2,1)S(1)} fusion(f32[256,864]{0,1:T(8,128)S(1)} %convolution_multiply_fusion.3, bf16[256,5120]{1,0:T(8,128)(2,1)S(1)} %get-tuple-element.46, bf16[5120,864]{1,0:T(8,128)(2,1)} %bitcast.204, f32[256,864]{0,1:T(8,128)} %fusion.60), kind=kOutput, calls=%fused_computation.55 | convolution fusion | flops 2266472448 | bytes 13680640 | tf_op jit(solution)/shard_map/dot_general | solution.py:16
  486.2 6.2 %fusion.32 = bf16[256,864]{0,1:T(8,128)(2,1)S(1)} fusion(f32[256,864]{0,1:T(8,128)S(1)} %convolution_multiply_fusion.2, bf16[256,5120]{1,0:T(8,128)(2,1)} %copy-done.9, bf16[5120,864]{1,0:T(8,128)(2,1)S(1)} %bitcast.192, f32[256,864]{0,1:T(8,128)} %fusion.60), kind=kOutput, calls=%fused_computation.56 | convolution fusion | flops 2266472448 | bytes 13680640 | tf_op jit(solution)/shard_map/dot_general | solution.py:16
  514.3 6.6 %fusion.61 = f32[256,864]{0,1:T(8,128)} fusion(bf16[256,5120]{1,0:T(8,128)(2,1)} %copy-done.16, bf16[5120,864]{1,0:T(8,128)(2,1)S(1)} %bitcast.201), kind=kOutput, calls=%fused_computation.186 | convolution fusion | flops 2264924160 | bytes 12353536 | tf_op jit(solution)/shard_map/dot_general | solution.py:16
  521.4 8.4 %fusion.33 = bf16[256,864]{0,1:T(8,128)(2,1)S(1)} fusion(f32[256,864]{0,1:T(8,128)S(1)} %convolution_multiply_fusion.1, bf16[256,5120]{1,0:T(8,128)(2,1)} %copy-done.16, bf16[5120,864]{1,0:T(8,128)(2,1)} %bitcast.205, f32[256,864]{0,1:T(8,128)} %fusion.61), kind=kOutput, calls=%fused_computation.57 | convolution fusion | flops 2266472448 | bytes 13680640 | tf_op jit(solution)/shard_map/dot_general | solution.py:16
  532.0 4.0 fusion.34
  539.4 15.5 %all_gather.19 = bf16[8,34,1024]{2,1,0:T(8,128)(2,1)S(1)} all-gather(bf16[1,34,1024]{2,1,0:T(8,128)(2,1)S(1)} %fusion.48), channel_id=1, replica_groups=mesh['o'=4,'i'=4,'mp'=2] {'o','mp'}, dimensions={0}, use_global_device_ids=true | all-gather | bytes 626688 | tf_op jit(solution)/shard_map/all_gather | solution.py:318
  574.6 7.9 %all_to_all.5 = bf16[4,16,1072]{2,1,0:T(8,128)(2,1)S(1)} all-to-all(bf16[4,16,1072]{2,1,0:T(8,128)(2,1)S(1)} %concatenate.48), channel_id=1, replica_groups=mesh['o'=4,'i'=4,'mp'=2] {'i'}, dimensions={0} | all-to-all | bytes 274432 | tf_op jit(solution)/shard_map/all_to_all | solution.py:353
  (307 shorter events, 154.6 us)
Async XLA Ops:
  0.6 184.4 %copy-start = (bf16[16,5120]{1,0:T(8,128)(2,1)S(1)}, bf16[16,5120]{1,0:T(8,128)(2,1)}, u32[]{:S(2)}) copy-start(bf16[16,5120]{1,0:T(8,128)(2,1)} %param.22) | copy-start | bytes 491524
  9.8 170.6 %collective-permute-start = (bf16[256,5120]{1,0:T(8,128)(2,1)S(1)}, bf16[256,5120]{1,0:T(8,128)(2,1)}, u32[]{:S(2)}, u32[]{:S(2)}) collective-permute-start(bf16[256,5120]{1,0:T(8,128)(2,1)S(1)} %pad_maximum_fusion.own), channel_id=1, source_target_pairs={{0,1},{1,0},{2,3},{3,2},{4,5},{5,4},{6,7},{7,6},{8,9},{9,8},{10,11... | collective-permute-start | bytes 7864328 | tf_op jit(solution)/shard_map/ppermute | solution.py:186
  10.2 174.3 %collective-permute-start.19 = (bf16[256,5120]{1,0:T(8,128)(2,1)S(1)}, bf16[256,5120]{1,0:T(8,128)(2,1)}, u32[]{:S(2)}, u32[]{:S(2)}) collective-permute-start(bf16[256,5120]{1,0:T(8,128)(2,1)S(1)} %pad_maximum_fusion.own), channel_id=1, source_target_pairs={{8,0},{16,8},{24,16},{9,1},{17,9},{25,17},{10,2},{18,10},{26,18},{... | collective-permute-start | bytes 7864328 | tf_op jit(solution)/shard_map/ppermute | solution.py:163
  11.6 174.2 %collective-permute-start.18 = (bf16[256,5120]{1,0:T(8,128)(2,1)S(1)}, bf16[256,5120]{1,0:T(8,128)(2,1)}, u32[]{:S(2)}, u32[]{:S(2)}) collective-permute-start(bf16[256,5120]{1,0:T(8,128)(2,1)S(1)} %pad_maximum_fusion.own), channel_id=1, source_target_pairs={{0,8},{8,16},{16,24},{1,9},{9,17},{17,25},{2,10},{10,18},{18,26},{... | collective-permute-start | bytes 7864328 | tf_op jit(solution)/shard_map/ppermute | solution.py:162
  18.4 68.0 %collective-permute-start.3 = (bf16[320,864]{1,0:T(8,128)(2,1)S(1)}, bf16[320,864]{1,0:T(8,128)(2,1)S(1)}, u32[]{:S(2)}, u32[]{:S(2)}) collective-permute-start(bf16[320,864]{1,0:T(8,128)(2,1)S(1)} %copy-done.37), channel_id=1, source_target_pairs={{0,24},{8,0},{16,8},{24,16},{1,25},{9,1},{17,9},{25,17},{2,26},{10... | collective-permute-start | bytes 1658888 | tf_op jit(solution)/shard_map/ppermute | solution.py:104
  22.4 76.3 %collective-permute-start.10 = (bf16[320,864]{1,0:T(8,128)(2,1)S(1)}, bf16[320,864]{1,0:T(8,128)(2,1)S(1)}, u32[]{:S(2)}, u32[]{:S(2)}) collective-permute-start(bf16[320,864]{1,0:T(8,128)(2,1)S(1)} %get-tuple-element.64), channel_id=1, source_target_pairs={{0,24},{8,0},{16,8},{24,16},{1,25},{9,1},{17,9},{25,17},{2,26},{10... | collective-permute-start | bytes 1658888 | tf_op jit(solution)/shard_map/ppermute | solution.py:104
  87.2 24.8 %collective-permute-start.8 = (bf16[320,864]{1,0:T(8,128)(2,1)S(1)}, bf16[320,864]{1,0:T(8,128)(2,1)S(1)}, u32[]{:S(2)}, u32[]{:S(2)}) collective-permute-start(bf16[320,864]{1,0:T(8,128)(2,1)S(1)} %get-tuple-element.65), channel_id=1, source_target_pairs={{0,8},{8,16},{16,24},{24,0},{1,9},{9,17},{17,25},{25,1},{2,10},{10... | collective-permute-start | bytes 1658888 | tf_op jit(solution)/shard_map/ppermute | solution.py:104
  99.6 61.0 %collective-permute-start.9 = (bf16[320,864]{1,0:T(8,128)(2,1)}, bf16[320,864]{1,0:T(8,128)(2,1)}, u32[]{:S(2)}, u32[]{:S(2)}) collective-permute-start(bf16[320,864]{1,0:T(8,128)(2,1)} %get-tuple-element.67), channel_id=1, source_target_pairs={{0,16},{8,24},{16,0},{24,8},{1,17},{9,25},{17,1},{25,9},{2,18},{10... | collective-permute-start | bytes 1658888 | tf_op jit(solution)/shard_map/ppermute | solution.py:104
  112.9 56.0 %collective-permute-start.1 = (bf16[320,864]{1,0:T(8,128)(2,1)}, bf16[320,864]{1,0:T(8,128)(2,1)}, u32[]{:S(2)}, u32[]{:S(2)}) collective-permute-start(bf16[320,864]{1,0:T(8,128)(2,1)} %get-tuple-element.73), channel_id=1, source_target_pairs={{0,8},{8,16},{16,24},{24,0},{1,9},{9,17},{17,25},{25,1},{2,10},{10... | collective-permute-start | bytes 1658888 | tf_op jit(solution)/shard_map/ppermute | solution.py:104
  160.6 16.1 %collective-permute-start.2 = (bf16[320,864]{1,0:T(8,128)(2,1)}, bf16[320,864]{1,0:T(8,128)(2,1)}, u32[]{:S(2)}, u32[]{:S(2)}) collective-permute-start(bf16[320,864]{1,0:T(8,128)(2,1)} %get-tuple-element.75), channel_id=1, source_target_pairs={{0,16},{8,24},{16,0},{24,8},{1,17},{9,25},{17,1},{25,9},{2,18},{10... | collective-permute-start | bytes 1658888 | tf_op jit(solution)/shard_map/ppermute | solution.py:104
  168.9 52.8 %collective-permute-start.13 = (bf16[4,320,864]{2,1,0:T(8,128)(2,1)S(1)}, bf16[4,320,864]{2,1,0:T(8,128)(2,1)S(1)}, u32[]{:S(2)}, u32[]{:S(2)}) collective-permute-start(bf16[4,320,864]{2,1,0:T(8,128)(2,1)S(1)} %shard_map.151.refs_0_), channel_id=1, source_target_pairs={{0,4},{2,6},{4,0},{6,2},{1,5},{3,7},{5,1},{7,3},{8,12},{10,14},{12... | collective-permute-start | bytes 6635528 | tf_op jit(solution)/shard_map/ppermute | solution.py:123
  176.7 52.7 %collective-permute-start.11 = (bf16[4,320,864]{2,1,0:T(8,128)(2,1)S(1)}, bf16[4,320,864]{2,1,0:T(8,128)(2,1)S(1)}, u32[]{:S(2)}, u32[]{:S(2)}) collective-permute-start(bf16[4,320,864]{2,1,0:T(8,128)(2,1)S(1)} %shard_map.151.refs_0_), channel_id=1, source_target_pairs={{0,2},{2,0},{4,6},{6,4},{1,3},{3,1},{5,7},{7,5},{8,10},{10,8},{12,... | collective-permute-start | bytes 6635528 | tf_op jit(solution)/shard_map/ppermute | solution.py:123
  180.4 89.5 %collective-permute-start.6 = (bf16[4,320,864]{2,1,0:T(8,128)(2,1)S(1)}, bf16[4,320,864]{2,1,0:T(8,128)(2,1)S(1)}, u32[]{:S(2)}, u32[]{:S(2)}) collective-permute-start(bf16[4,320,864]{2,1,0:T(8,128)(2,1)S(1)} %shard_map.148.refs_0_), channel_id=1, source_target_pairs={{0,4},{2,6},{4,0},{6,2},{1,5},{3,7},{5,1},{7,3},{8,12},{10,14},{12... | collective-permute-start | bytes 6635528 | tf_op jit(solution)/shard_map/ppermute | solution.py:123
  184.5 94.1 %collective-permute-start.4 = (bf16[4,320,864]{2,1,0:T(8,128)(2,1)S(1)}, bf16[4,320,864]{2,1,0:T(8,128)(2,1)S(1)}, u32[]{:S(2)}, u32[]{:S(2)}) collective-permute-start(bf16[4,320,864]{2,1,0:T(8,128)(2,1)S(1)} %shard_map.148.refs_0_), channel_id=1, source_target_pairs={{0,2},{2,0},{4,6},{6,4},{1,3},{3,1},{5,7},{7,5},{8,10},{10,8},{12,... | collective-permute-start | bytes 6635528 | tf_op jit(solution)/shard_map/ppermute | solution.py:123
  185.8 94.3 %collective-permute-start.17 = (bf16[320,864]{1,0:T(8,128)(2,1)S(1)}, bf16[320,864]{1,0:T(8,128)(2,1)S(1)}, u32[]{:S(2)}, u32[]{:S(2)}) collective-permute-start(bf16[320,864]{1,0:T(8,128)(2,1)S(1)} %get-tuple-element.68), channel_id=1, source_target_pairs={{0,24},{8,0},{16,8},{24,16},{1,25},{9,1},{17,9},{25,17},{2,26},{10... | collective-permute-start | bytes 1658888 | tf_op jit(solution)/shard_map/ppermute | solution.py:104
  221.7 62.2 %collective-permute-start.15 = (bf16[320,864]{1,0:T(8,128)(2,1)S(1)}, bf16[320,864]{1,0:T(8,128)(2,1)S(1)}, u32[]{:S(2)}, u32[]{:S(2)}) collective-permute-start(bf16[320,864]{1,0:T(8,128)(2,1)S(1)} %get-tuple-element.69), channel_id=1, source_target_pairs={{0,8},{8,16},{16,24},{24,0},{1,9},{9,17},{17,25},{25,1},{2,10},{10... | collective-permute-start | bytes 1658888 | tf_op jit(solution)/shard_map/ppermute | solution.py:104
  229.4 73.7 %collective-permute-start.14 = (bf16[2,320,864]{2,1,0:T(8,128)(2,1)S(1)}, bf16[2,320,864]{2,1,0:T(8,128)(2,1)S(1)}, u32[]{:S(2)}, u32[]{:S(2)}) collective-permute-start(bf16[2,320,864]{2,1,0:T(8,128)(2,1)S(1)} %slice.121), channel_id=1, source_target_pairs={{0,2},{2,0},{4,6},{6,4},{1,3},{3,1},{5,7},{7,5},{8,10},{10,8},{12,... | collective-permute-start | bytes 3317768 | tf_op jit(solution)/shard_map/ppermute | solution.py:134
  269.9 34.5 %collective-permute-start.12 = (bf16[2,320,864]{2,1,0:T(8,128)(2,1)}, bf16[2,320,864]{2,1,0:T(8,128)(2,1)S(1)}, u32[]{:S(2)}, u32[]{:S(2)}) collective-permute-start(bf16[2,320,864]{2,1,0:T(8,128)(2,1)} %slice.120), channel_id=1, source_target_pairs={{0,4},{2,6},{4,0},{6,2},{1,5},{3,7},{5,1},{7,3},{8,12},{10,14},{12... | collective-permute-start | bytes 3317768 | tf_op jit(solution)/shard_map/ppermute | solution.py:134
  278.6 47.3 %collective-permute-start.7 = (bf16[2,320,864]{2,1,0:T(8,128)(2,1)S(1)}, bf16[2,320,864]{2,1,0:T(8,128)(2,1)S(1)}, u32[]{:S(2)}, u32[]{:S(2)}) collective-permute-start(bf16[2,320,864]{2,1,0:T(8,128)(2,1)S(1)} %slice.119), channel_id=1, source_target_pairs={{0,2},{2,0},{4,6},{6,4},{1,3},{3,1},{5,7},{7,5},{8,10},{10,8},{12,... | collective-permute-start | bytes 3317768 | tf_op jit(solution)/shard_map/ppermute | solution.py:134
  280.2 47.3 %collective-permute-start.5 = (bf16[2,320,864]{2,1,0:T(8,128)(2,1)S(1)}, bf16[2,320,864]{2,1,0:T(8,128)(2,1)S(1)}, u32[]{:S(2)}, u32[]{:S(2)}) collective-permute-start(bf16[2,320,864]{2,1,0:T(8,128)(2,1)S(1)} %slice.118), channel_id=1, source_target_pairs={{0,4},{2,6},{4,0},{6,2},{1,5},{3,7},{5,1},{7,3},{8,12},{10,14},{12... | collective-permute-start | bytes 3317768 | tf_op jit(solution)/shard_map/ppermute | solution.py:134
  283.9 11.7 %collective-permute-start.16 = (bf16[320,864]{1,0:T(8,128)(2,1)S(1)}, bf16[320,864]{1,0:T(8,128)(2,1)S(1)}, u32[]{:S(2)}, u32[]{:S(2)}) collective-permute-start(bf16[320,864]{1,0:T(8,128)(2,1)S(1)} %get-tuple-element.71), channel_id=1, source_target_pairs={{0,16},{8,24},{16,0},{24,8},{1,17},{9,25},{17,1},{25,9},{2,18},{10... | collective-permute-start | bytes 1658888 | tf_op jit(solution)/shard_map/ppermute | solution.py:104
  295.7 91.9 %collective-permute-start.24 = (bf16[256,5120]{1,0:T(8,128)(2,1)}, bf16[256,5120]{1,0:T(8,128)(2,1)}, u32[]{:S(2)}, u32[]{:S(2)}) collective-permute-start(bf16[256,5120]{1,0:T(8,128)(2,1)} %broadcast_select_fusion.1.own), channel_id=1, source_target_pairs={{0,1},{1,0},{2,3},{3,2},{4,5},{5,4},{6,7},{7,6},{8,9},{9,8},{10,11... | collective-permute-start | bytes 7864328 | tf_op jit(solution)/shard_map/ppermute | solution.py:186
  303.2 108.3 %collective-permute-start.25 = (bf16[256,5120]{1,0:T(8,128)(2,1)}, bf16[256,5120]{1,0:T(8,128)(2,1)}, u32[]{:S(2)}, u32[]{:S(2)}) collective-permute-start(bf16[256,5120]{1,0:T(8,128)(2,1)} %collective-permute-done.19), channel_id=1, source_target_pairs={{8,0},{16,8},{9,1},{17,9},{10,2},{18,10},{11,3},{19,11},{12,4},{20... | collective-permute-start | bytes 7864328 | tf_op jit(solution)/shard_map/ppermute | solution.py:163
  304.5 107.0 %collective-permute-start.26 = (bf16[256,5120]{1,0:T(8,128)(2,1)}, bf16[256,5120]{1,0:T(8,128)(2,1)}, u32[]{:S(2)}, u32[]{:S(2)}) collective-permute-start(bf16[256,5120]{1,0:T(8,128)(2,1)} %collective-permute-done.18), channel_id=1, source_target_pairs={{8,16},{16,24},{9,17},{17,25},{10,18},{18,26},{11,19},{19,27},{12,... | collective-permute-start | bytes 7864328 | tf_op jit(solution)/shard_map/ppermute | solution.py:162
  325.9 50.3 %collective-permute-start.22 = (bf16[4,320,864]{2,1,0:T(8,128)(2,1)S(1)}, bf16[4,320,864]{2,1,0:T(8,128)(2,1)}, u32[]{:S(2)}, u32[]{:S(2)}) collective-permute-start(bf16[4,320,864]{2,1,0:T(8,128)(2,1)S(1)} %shard_map.154.refs_0_), channel_id=1, source_target_pairs={{0,4},{2,6},{4,0},{6,2},{1,5},{3,7},{5,1},{7,3},{8,12},{10,14},{12... | collective-permute-start | bytes 6635528 | tf_op jit(solution)/shard_map/ppermute | solution.py:123
  327.5 52.6 %collective-permute-start.20 = (bf16[4,320,864]{2,1,0:T(8,128)(2,1)S(1)}, bf16[4,320,864]{2,1,0:T(8,128)(2,1)}, u32[]{:S(2)}, u32[]{:S(2)}) collective-permute-start(bf16[4,320,864]{2,1,0:T(8,128)(2,1)S(1)} %shard_map.154.refs_0_), channel_id=1, source_target_pairs={{0,2},{2,0},{4,6},{6,4},{1,3},{3,1},{5,7},{7,5},{8,10},{10,8},{12,... | collective-permute-start | bytes 6635528 | tf_op jit(solution)/shard_map/ppermute | solution.py:123
  378.6 43.1 %collective-permute-start.23 = (bf16[2,320,864]{2,1,0:T(8,128)(2,1)}, bf16[2,320,864]{2,1,0:T(8,128)(2,1)}, u32[]{:S(2)}, u32[]{:S(2)}) collective-permute-start(bf16[2,320,864]{2,1,0:T(8,128)(2,1)} %slice.123), channel_id=1, source_target_pairs={{0,2},{2,0},{4,6},{6,4},{1,3},{3,1},{5,7},{7,5},{8,10},{10,8},{12,... | collective-permute-start | bytes 3317768 | tf_op jit(solution)/shard_map/ppermute | solution.py:134
  382.4 39.3 %collective-permute-start.21 = (bf16[2,320,864]{2,1,0:T(8,128)(2,1)}, bf16[2,320,864]{2,1,0:T(8,128)(2,1)}, u32[]{:S(2)}, u32[]{:S(2)}) collective-permute-start(bf16[2,320,864]{2,1,0:T(8,128)(2,1)} %slice.122), channel_id=1, source_target_pairs={{0,4},{2,6},{4,0},{6,2},{1,5},{3,7},{5,1},{7,3},{8,12},{10,14},{12... | collective-permute-start | bytes 3317768 | tf_op jit(solution)/shard_map/ppermute | solution.py:134
  413.9 31.6 %collective-permute-start.27 = (bf16[256,5120]{1,0:T(8,128)(2,1)S(1)}, bf16[256,5120]{1,0:T(8,128)(2,1)}, u32[]{:S(2)}, u32[]{:S(2)}) collective-permute-start(bf16[256,5120]{1,0:T(8,128)(2,1)S(1)} %broadcast_select_fusion.own), channel_id=1, source_target_pairs={{0,1},{1,0},{2,3},{3,2},{4,5},{5,4},{6,7},{7,6},{8,9},{9,8},{10,11... | collective-permute-start | bytes 7864328 | tf_op jit(solution)/shard_map/ppermute | solution.py:186
  413.9 61.5 %collective-permute-start.28 = (bf16[256,5120]{1,0:T(8,128)(2,1)}, bf16[256,5120]{1,0:T(8,128)(2,1)}, u32[]{:S(2)}, u32[]{:S(2)}) collective-permute-start(bf16[256,5120]{1,0:T(8,128)(2,1)} %collective-permute-done.25), channel_id=1, source_target_pairs={{8,0},{9,1},{10,2},{11,3},{12,4},{13,5},{14,6},{15,7}} | collective-permute-start | bytes 7864328 | tf_op jit(solution)/shard_map/ppermute | solution.py:163
  415.2 60.2 %collective-permute-start.29 = (bf16[256,5120]{1,0:T(8,128)(2,1)}, bf16[256,5120]{1,0:T(8,128)(2,1)}, u32[]{:S(2)}, u32[]{:S(2)}) collective-permute-start(bf16[256,5120]{1,0:T(8,128)(2,1)} %collective-permute-done.26), channel_id=1, source_target_pairs={{16,24},{17,25},{18,26},{19,27},{20,28},{21,29},{22,30},{23,31}} | collective-permute-start | bytes 7864328 | tf_op jit(solution)/shard_map/ppermute | solution.py:162
  477.8 28.7 %collective-permute-start.30 = (bf16[256,5120]{1,0:T(8,128)(2,1)S(1)}, bf16[256,5120]{1,0:T(8,128)(2,1)}, u32[]{:S(2)}, u32[]{:S(2)}) collective-permute-start(bf16[256,5120]{1,0:T(8,128)(2,1)S(1)} %select_select_fusion.own), channel_id=1, source_target_pairs={{0,1},{1,0},{2,3},{3,2},{4,5},{5,4},{6,7},{7,6},{8,9},{9,8},{10,11... | collective-permute-start | bytes 7864328 | tf_op jit(solution)/shard_map/ppermute | solution.py:186
  (59 other events, 754.4 us)

commit v2 on v1

--- a/solution.py
+++ b/solution.py
@@ -348,8 +348,11 @@
         clipped(grad_down_first),
         token_gradient(lat_down, grad_share),
     )
-    pieces = [a.reshape(rank, p, size).swapaxes(0, 1) for a, size in zip(pieces, sizes)]
-    pieces = jnp.concatenate(pieces, axis=2).astype(bf16)
+    pieces = [a.astype(bf16) for a in pieces]
+    pieces = jnp.concatenate(
+        [a[:, j * size : (j + 1) * size] for j in range(p) for a, size in zip(pieces, sizes)], axis=1
+    )
+    pieces = pieces.reshape(rank, p, -1).swapaxes(0, 1)
     total = lax.all_to_all(pieces, "i", 0, 0, tiled=True)
     total = jnp.sum(total.reshape(p, rank, -1).astype(f32), axis=0)
     outs, start = [], 0

time: 595 us -> 589 us (0.990)
  no operation moved by 1% of the time
where the time goes in v2:
time: 589 us; the launch traced here: 579 us
  waiting for transfers between devices  289 us (49%)
  matrix products  132 us (22%)
  starting transfers between devices  41.7 us (7%)
  local copies, waits for them, and re-layouts  38 us (6%)
  Pallas kernels  26.6 us (5%)
  blocking collectives  26 us (4%)
  between operations  13.3 us (2%)
  other arithmetic  13 us (2%)
    ppermute x9, waiting for transfers between devices, exchange(): lax.ppermute(pieces[d], 'o', [(s, (s + d) % r) for s in range(r)])  141 us
    ppermute x6, waiting for transfers between devices, neighbours(): lax.ppermute(part, 'i', [(s, s ^ bit) for s in range(p)])  111 us
    dot_general x22, matrix products, matmul(): return jnp.dot(left, right, preferred_element_type=jnp.float32)  97.6 us
    dot_general x32, matrix products, contract(): lax.dot_general(left, right, (((left_dim,), (right_dim,)), ((), ())), pre...  32.8 us
    ppermute x6, waiting for transfers between devices, assembled(): lax.ppermute(piece, 'i', [(s, s ^ bit) for s in range(p)])  20.3 us
    ppermute x3, waiting for transfers between devices, gather_path(): lax.ppermute(down[-1], 'o', [(s, s - 1) for s in range(1, r - k + 1)])  15.7 us
    all_gather x1, blocking collectives, per_device(): lax.all_gather(sums, ('o', 'mp'), axis=0).astype(f32)  15.5 us
  transfers between devices with their start and end apart: 31, of which 14 were waited for; matrix products, arithmetic and copies ran while one was open for 22% of the time, Pallas kernels for 4%

profile of v2, /device:TPU:0, one launch (start us, length us, event | category | flops | bytes accessed | tf_op | source)
XLA Modules:
  0.0 578.8 jit_solution(12058545294669588202)
XLA Ops:
  1.5 4.2 constant_dynamic-slice_fusion.22
  11.6 6.8 %collective-permute-start.18 = (bf16[256,5120]{1,0:T(8,128)(2,1)S(1)}, bf16[256,5120]{1,0:T(8,128)(2,1)}, u32[]{:S(2)}, u32[]{:S(2)}) collective-permute-start(bf16[256,5120]{1,0:T(8,128)(2,1)S(1)} %pad_maximum_fusion.own), channel_id=1, source_target_pairs={{0,8},{8,16},{16,24},{1,9},{9,17},{17,25},{2,10},{10,18},{18,26},{... | collective-permute-start | bytes 7864328 | tf_op jit(solution)/shard_map/ppermute | solution.py:162
  25.1 61.3 %collective-permute-done.3.refs_3_ = bf16[320,864]{1,0:T(8,128)(2,1)S(1)} collective-permute-done((bf16[320,864]{1,0:T(8,128)(2,1)S(1)}, bf16[320,864]{1,0:T(8,128)(2,1)S(1)}, u32[]{:S(2)}, u32[]{:S(2)}) %collective-permute-start.3) | collective-permute-done | bytes 552992 | tf_op jit(solution)/shard_map/ppermute | solution.py:104
  87.8 10.9 %collective-permute-done.10.refs_3_ = bf16[320,864]{1,0:T(8,128)(2,1)S(1)} collective-permute-done((bf16[320,864]{1,0:T(8,128)(2,1)S(1)}, bf16[320,864]{1,0:T(8,128)(2,1)S(1)}, u32[]{:S(2)}, u32[]{:S(2)}) %collective-permute-start.10) | collective-permute-done | bytes 552992 | tf_op jit(solution)/shard_map/ppermute | solution.py:104
  101.1 11.0 %collective-permute-done.8.refs_1_ = bf16[320,864]{1,0:T(8,128)(2,1)S(1)} collective-permute-done((bf16[320,864]{1,0:T(8,128)(2,1)S(1)}, bf16[320,864]{1,0:T(8,128)(2,1)S(1)}, u32[]{:S(2)}, u32[]{:S(2)}) %collective-permute-start.8) | collective-permute-done | bytes 552992 | tf_op jit(solution)/shard_map/ppermute | solution.py:104
  115.0 45.6 %collective-permute-done.9.refs_2_ = bf16[320,864]{1,0:T(8,128)(2,1)} collective-permute-done((bf16[320,864]{1,0:T(8,128)(2,1)}, bf16[320,864]{1,0:T(8,128)(2,1)}, u32[]{:S(2)}, u32[]{:S(2)}) %collective-permute-start.9) | collective-permute-done | bytes 552992 | tf_op jit(solution)/shard_map/ppermute | solution.py:104
  171.9 4.8 collective-permute-done.2.refs_2_
  185.9 3.9 broadcast_select_fusion.1.own
  190.7 31.2 %collective-permute-done.13.refs_2_ = bf16[4,320,864]{2,1,0:T(8,128)(2,1)S(1)} collective-permute-done((bf16[4,320,864]{2,1,0:T(8,128)(2,1)S(1)}, bf16[4,320,864]{2,1,0:T(8,128)(2,1)S(1)}, u32[]{:S(2)}, u32[]{:S(2)}) %collective-permute-start.13) | collective-permute-done | bytes 2211872 | tf_op jit(solution)/shard_map/ppermute | solution.py:123
  223.6 5.8 %collective-permute-done.11.refs_1_ = bf16[4,320,864]{2,1,0:T(8,128)(2,1)S(1)} collective-permute-done((bf16[4,320,864]{2,1,0:T(8,128)(2,1)S(1)}, bf16[4,320,864]{2,1,0:T(8,128)(2,1)S(1)}, u32[]{:S(2)}, u32[]{:S(2)}) %collective-permute-start.11) | collective-permute-done | bytes 2211872 | tf_op jit(solution)/shard_map/ppermute | solution.py:123
  232.0 38.0 %collective-permute-done.6.refs_2_ = bf16[4,320,864]{2,1,0:T(8,128)(2,1)S(1)} collective-permute-done((bf16[4,320,864]{2,1,0:T(8,128)(2,1)S(1)}, bf16[4,320,864]{2,1,0:T(8,128)(2,1)S(1)}, u32[]{:S(2)}, u32[]{:S(2)}) %collective-permute-start.6) | collective-permute-done | bytes 2211872 | tf_op jit(solution)/shard_map/ppermute | solution.py:123
  271.7 6.9 %collective-permute-done.4.refs_1_ = bf16[4,320,864]{2,1,0:T(8,128)(2,1)S(1)} collective-permute-done((bf16[4,320,864]{2,1,0:T(8,128)(2,1)S(1)}, bf16[4,320,864]{2,1,0:T(8,128)(2,1)S(1)}, u32[]{:S(2)}, u32[]{:S(2)}) %collective-permute-start.4) | collective-permute-done | bytes 2211872 | tf_op jit(solution)/shard_map/ppermute | solution.py:123
  288.0 7.7 %collective-permute-done.16.refs_2_ = bf16[320,864]{1,0:T(8,128)(2,1)S(1)} collective-permute-done((bf16[320,864]{1,0:T(8,128)(2,1)S(1)}, bf16[320,864]{1,0:T(8,128)(2,1)S(1)}, u32[]{:S(2)}, u32[]{:S(2)}) %collective-permute-start.16) | collective-permute-done | bytes 552992 | tf_op jit(solution)/shard_map/ppermute | solution.py:104
  307.7 18.2 %collective-permute-done.7.refs_1_ = bf16[2,320,864]{2,1,0:T(8,128)(2,1)S(1)} collective-permute-done((bf16[2,320,864]{2,1,0:T(8,128)(2,1)S(1)}, bf16[2,320,864]{2,1,0:T(8,128)(2,1)S(1)}, u32[]{:S(2)}, u32[]{:S(2)}) %collective-permute-start.7) | collective-permute-done | bytes 1105952 | tf_op jit(solution)/shard_map/ppermute | solution.py:134
  329.8 8.4 %fusion.62 = f32[256,864]{0,1:T(8,128)} fusion(bf16[256,5120]{1,0:T(8,128)(2,1)} %copy-done.6, bf16[5120,864]{1,0:T(8,128)(2,1)S(1)} %bitcast.187), kind=kOutput, calls=%fused_computation.184 | convolution fusion | flops 2264924160 | bytes 12353536 | tf_op jit(solution)/shard_map/dot_general | solution.py:16
  338.2 6.0 %fusion.27 = bf16[256,864]{0,1:T(8,128)(2,1)S(1)} fusion(f32[256,864]{0,1:T(8,128)} %convolution_multiply_fusion.7, bf16[256,5120]{1,0:T(8,128)(2,1)} %copy-done.6, bf16[5120,864]{1,0:T(8,128)(2,1)S(1)} %bitcast.193, f32[256,864]{0,1:T(8,128)} %fusion.62), kind=kOutput, calls=%fused_computation.51 | convolution fusion | flops 2266472448 | bytes 13680640 | tf_op jit(solution)/shard_map/dot_general | solution.py:16
  346.7 29.5 %collective-permute-done.22.refs_2_ = bf16[4,320,864]{2,1,0:T(8,128)(2,1)} collective-permute-done((bf16[4,320,864]{2,1,0:T(8,128)(2,1)S(1)}, bf16[4,320,864]{2,1,0:T(8,128)(2,1)}, u32[]{:S(2)}, u32[]{:S(2)}) %collective-permute-start.22) | collective-permute-done | bytes 2211872 | tf_op jit(solution)/shard_map/ppermute | solution.py:123
  383.9 3.6 shard_map.155.refs_2_
  387.6 3.1 shard_map.157
  393.5 7.3 %fusion.63 = f32[256,864]{0,1:T(8,128)S(1)} fusion(bf16[256,5120]{1,0:T(8,128)(2,1)S(1)} %get-tuple-element.42, bf16[5120,864]{1,0:T(8,128)(2,1)} %bitcast.188), kind=kOutput, calls=%fused_computation.185 | convolution fusion | flops 2264924160 | bytes 12353536 | tf_op jit(solution)/shard_map/dot_general | solution.py:16
  400.9 7.7 %fusion.29 = bf16[256,864]{0,1:T(8,128)(2,1)S(1)} fusion(f32[256,864]{0,1:T(8,128)S(1)} %convolution_multiply_fusion.5, bf16[256,5120]{1,0:T(8,128)(2,1)S(1)} %get-tuple-element.42, bf16[5120,864]{1,0:T(8,128)(2,1)} %bitcast.194, f32[256,864]{0,1:T(8,128)S(1)} %fusion.63), kind=kOutput, calls=%fused_computation.53 | convolution fusion | flops 2266472448 | bytes 13680640 | tf_op jit(solution)/shard_map/dot_general | solution.py:16
  423.9 8.5 %fusion.30 = bf16[256,864]{0,1:T(8,128)(2,1)S(1)} fusion(f32[256,864]{0,1:T(8,128)S(1)} %convolution_multiply_fusion.4, bf16[256,5120]{1,0:T(8,128)(2,1)} %copy-done.11, bf16[5120,864]{1,0:T(8,128)(2,1)S(1)} %bitcast.179, f32[256,864]{0,1:T(8,128)} %copy-done.52), kind=kOutput, calls=%fused_computation.54 | convolution fusion | flops 2266472448 | bytes 13680640 | tf_op jit(solution)/shard_map/dot_general | solution.py:16
  433.9 5.0 fusion.28
  451.4 8.2 %fusion.64 = f32[256,864]{0,1:T(8,128)} fusion(bf16[256,5120]{1,0:T(8,128)(2,1)S(1)} %get-tuple-element.46, bf16[5120,864]{1,0:T(8,128)(2,1)} %bitcast.189), kind=kOutput, calls=%fused_computation.186 | convolution fusion | flops 2264924160 | bytes 12353536 | tf_op jit(solution)/shard_map/dot_general | solution.py:16
  459.7 15.7 %collective-permute-done.28 = bf16[256,5120]{1,0:T(8,128)(2,1)} collective-permute-done((bf16[256,5120]{1,0:T(8,128)(2,1)}, bf16[256,5120]{1,0:T(8,128)(2,1)}, u32[]{:S(2)}, u32[]{:S(2)}) %collective-permute-start.28) | collective-permute-done | bytes 2621472 | tf_op jit(solution)/shard_map/ppermute | solution.py:163
  477.9 8.3 %fusion.31 = bf16[256,864]{0,1:T(8,128)(2,1)S(1)} fusion(f32[256,864]{0,1:T(8,128)S(1)} %convolution_multiply_fusion.3, bf16[256,5120]{1,0:T(8,128)(2,1)S(1)} %get-tuple-element.46, bf16[5120,864]{1,0:T(8,128)(2,1)} %bitcast.195, f32[256,864]{0,1:T(8,128)} %fusion.64), kind=kOutput, calls=%fused_computation.55 | convolution fusion | flops 2266472448 | bytes 13680640 | tf_op jit(solution)/shard_map/dot_general | solution.py:16
  486.2 6.2 %fusion.32 = bf16[256,864]{0,1:T(8,128)(2,1)S(1)} fusion(f32[256,864]{0,1:T(8,128)S(1)} %convolution_multiply_fusion.2, bf16[256,5120]{1,0:T(8,128)(2,1)} %copy-done.9, bf16[5120,864]{1,0:T(8,128)(2,1)S(1)} %bitcast.183, f32[256,864]{0,1:T(8,128)} %fusion.64), kind=kOutput, calls=%fused_computation.56 | convolution fusion | flops 2266472448 | bytes 13680640 | tf_op jit(solution)/shard_map/dot_general | solution.py:16
  514.2 6.6 %fusion.65 = f32[256,864]{0,1:T(8,128)} fusion(bf16[256,5120]{1,0:T(8,128)(2,1)} %copy-done.16, bf16[5120,864]{1,0:T(8,128)(2,1)S(1)} %bitcast.192), kind=kOutput, calls=%fused_computation.187 | convolution fusion | flops 2264924160 | bytes 12353536 | tf_op jit(solution)/shard_map/dot_general | solution.py:16
  521.3 8.4 %fusion.33 = bf16[256,864]{0,1:T(8,128)(2,1)S(1)} fusion(f32[256,864]{0,1:T(8,128)S(1)} %convolution_multiply_fusion.1, bf16[256,5120]{1,0:T(8,128)(2,1)} %copy-done.16, bf16[5120,864]{1,0:T(8,128)(2,1)} %bitcast.196, f32[256,864]{0,1:T(8,128)} %fusion.65), kind=kOutput, calls=%fused_computation.57 | convolution fusion | flops 2266472448 | bytes 13680640 | tf_op jit(solution)/shard_map/dot_general | solution.py:16
  532.0 4.0 fusion.34
  539.3 15.5 %all_gather.19 = bf16[8,34,1024]{2,1,0:T(8,128)(2,1)S(1)} all-gather(bf16[1,34,1024]{2,1,0:T(8,128)(2,1)S(1)} %fusion.48), channel_id=1, replica_groups=mesh['o'=4,'i'=4,'mp'=2] {'o','mp'}, dimensions={0}, use_global_device_ids=true | all-gather | bytes 626688 | tf_op jit(solution)/shard_map/all_gather | solution.py:318
  569.3 7.9 %all_to_all.5 = bf16[4,16,1072]{2,1,0:T(8,128)(2,1)S(1)} all-to-all(bf16[4,16,1072]{2,1,0:T(8,128)(2,1)S(1)} %bitcast.197), channel_id=1, replica_groups=mesh['o'=4,'i'=4,'mp'=2] {'i'}, dimensions={0} | all-to-all | bytes 274432 | tf_op jit(solution)/shard_map/all_to_all | solution.py:356
  (311 shorter events, 149.2 us)
Async XLA Ops:
  0.6 184.4 %copy-start = (bf16[16,5120]{1,0:T(8,128)(2,1)S(1)}, bf16[16,5120]{1,0:T(8,128)(2,1)}, u32[]{:S(2)}) copy-start(bf16[16,5120]{1,0:T(8,128)(2,1)} %param.22) | copy-start | bytes 491524
  9.8 170.6 %collective-permute-start = (bf16[256,5120]{1,0:T(8,128)(2,1)S(1)}, bf16[256,5120]{1,0:T(8,128)(2,1)}, u32[]{:S(2)}, u32[]{:S(2)}) collective-permute-start(bf16[256,5120]{1,0:T(8,128)(2,1)S(1)} %pad_maximum_fusion.own), channel_id=1, source_target_pairs={{0,1},{1,0},{2,3},{3,2},{4,5},{5,4},{6,7},{7,6},{8,9},{9,8},{10,11... | collective-permute-start | bytes 7864328 | tf_op jit(solution)/shard_map/ppermute | solution.py:186
  10.2 174.3 %collective-permute-start.19 = (bf16[256,5120]{1,0:T(8,128)(2,1)S(1)}, bf16[256,5120]{1,0:T(8,128)(2,1)}, u32[]{:S(2)}, u32[]{:S(2)}) collective-permute-start(bf16[256,5120]{1,0:T(8,128)(2,1)S(1)} %pad_maximum_fusion.own), channel_id=1, source_target_pairs={{8,0},{16,8},{24,16},{9,1},{17,9},{25,17},{10,2},{18,10},{26,18},{... | collective-permute-start | bytes 7864328 | tf_op jit(solution)/shard_map/ppermute | solution.py:163
  11.6 174.2 %collective-permute-start.18 = (bf16[256,5120]{1,0:T(8,128)(2,1)S(1)}, bf16[256,5120]{1,0:T(8,128)(2,1)}, u32[]{:S(2)}, u32[]{:S(2)}) collective-permute-start(bf16[256,5120]{1,0:T(8,128)(2,1)S(1)} %pad_maximum_fusion.own), channel_id=1, source_target_pairs={{0,8},{8,16},{16,24},{1,9},{9,17},{17,25},{2,10},{10,18},{18,26},{... | collective-permute-start | bytes 7864328 | tf_op jit(solution)/shard_map/ppermute | solution.py:162
  18.4 68.0 %collective-permute-start.3 = (bf16[320,864]{1,0:T(8,128)(2,1)S(1)}, bf16[320,864]{1,0:T(8,128)(2,1)S(1)}, u32[]{:S(2)}, u32[]{:S(2)}) collective-permute-start(bf16[320,864]{1,0:T(8,128)(2,1)S(1)} %copy-done.37), channel_id=1, source_target_pairs={{0,24},{8,0},{16,8},{24,16},{1,25},{9,1},{17,9},{25,17},{2,26},{10... | collective-permute-start | bytes 1658888 | tf_op jit(solution)/shard_map/ppermute | solution.py:104
  22.5 76.3 %collective-permute-start.10 = (bf16[320,864]{1,0:T(8,128)(2,1)S(1)}, bf16[320,864]{1,0:T(8,128)(2,1)S(1)}, u32[]{:S(2)}, u32[]{:S(2)}) collective-permute-start(bf16[320,864]{1,0:T(8,128)(2,1)S(1)} %get-tuple-element.64), channel_id=1, source_target_pairs={{0,24},{8,0},{16,8},{24,16},{1,25},{9,1},{17,9},{25,17},{2,26},{10... | collective-permute-start | bytes 1658888 | tf_op jit(solution)/shard_map/ppermute | solution.py:104
  87.3 24.8 %collective-permute-start.8 = (bf16[320,864]{1,0:T(8,128)(2,1)S(1)}, bf16[320,864]{1,0:T(8,128)(2,1)S(1)}, u32[]{:S(2)}, u32[]{:S(2)}) collective-permute-start(bf16[320,864]{1,0:T(8,128)(2,1)S(1)} %get-tuple-element.65), channel_id=1, source_target_pairs={{0,8},{8,16},{16,24},{24,0},{1,9},{9,17},{17,25},{25,1},{2,10},{10... | collective-permute-start | bytes 1658888 | tf_op jit(solution)/shard_map/ppermute | solution.py:104
  99.6 61.0 %collective-permute-start.9 = (bf16[320,864]{1,0:T(8,128)(2,1)}, bf16[320,864]{1,0:T(8,128)(2,1)}, u32[]{:S(2)}, u32[]{:S(2)}) collective-permute-start(bf16[320,864]{1,0:T(8,128)(2,1)} %get-tuple-element.67), channel_id=1, source_target_pairs={{0,16},{8,24},{16,0},{24,8},{1,17},{9,25},{17,1},{25,9},{2,18},{10... | collective-permute-start | bytes 1658888 | tf_op jit(solution)/shard_map/ppermute | solution.py:104
  112.9 56.1 %collective-permute-start.1 = (bf16[320,864]{1,0:T(8,128)(2,1)}, bf16[320,864]{1,0:T(8,128)(2,1)}, u32[]{:S(2)}, u32[]{:S(2)}) collective-permute-start(bf16[320,864]{1,0:T(8,128)(2,1)} %get-tuple-element.73), channel_id=1, source_target_pairs={{0,8},{8,16},{16,24},{24,0},{1,9},{9,17},{17,25},{25,1},{2,10},{10... | collective-permute-start | bytes 1658888 | tf_op jit(solution)/shard_map/ppermute | solution.py:104
  160.6 16.1 %collective-permute-start.2 = (bf16[320,864]{1,0:T(8,128)(2,1)}, bf16[320,864]{1,0:T(8,128)(2,1)}, u32[]{:S(2)}, u32[]{:S(2)}) collective-permute-start(bf16[320,864]{1,0:T(8,128)(2,1)} %get-tuple-element.75), channel_id=1, source_target_pairs={{0,16},{8,24},{16,0},{24,8},{1,17},{9,25},{17,1},{25,9},{2,18},{10... | collective-permute-start | bytes 1658888 | tf_op jit(solution)/shard_map/ppermute | solution.py:104
  169.1 52.8 %collective-permute-start.13 = (bf16[4,320,864]{2,1,0:T(8,128)(2,1)S(1)}, bf16[4,320,864]{2,1,0:T(8,128)(2,1)S(1)}, u32[]{:S(2)}, u32[]{:S(2)}) collective-permute-start(bf16[4,320,864]{2,1,0:T(8,128)(2,1)S(1)} %shard_map.151.refs_0_), channel_id=1, source_target_pairs={{0,4},{2,6},{4,0},{6,2},{1,5},{3,7},{5,1},{7,3},{8,12},{10,14},{12... | collective-permute-start | bytes 6635528 | tf_op jit(solution)/shard_map/ppermute | solution.py:123
  176.7 52.7 %collective-permute-start.11 = (bf16[4,320,864]{2,1,0:T(8,128)(2,1)S(1)}, bf16[4,320,864]{2,1,0:T(8,128)(2,1)S(1)}, u32[]{:S(2)}, u32[]{:S(2)}) collective-permute-start(bf16[4,320,864]{2,1,0:T(8,128)(2,1)S(1)} %shard_map.151.refs_0_), channel_id=1, source_target_pairs={{0,2},{2,0},{4,6},{6,4},{1,3},{3,1},{5,7},{7,5},{8,10},{10,8},{12,... | collective-permute-start | bytes 6635528 | tf_op jit(solution)/shard_map/ppermute | solution.py:123
  180.4 89.7 %collective-permute-start.6 = (bf16[4,320,864]{2,1,0:T(8,128)(2,1)S(1)}, bf16[4,320,864]{2,1,0:T(8,128)(2,1)S(1)}, u32[]{:S(2)}, u32[]{:S(2)}) collective-permute-start(bf16[4,320,864]{2,1,0:T(8,128)(2,1)S(1)} %shard_map.148.refs_0_), channel_id=1, source_target_pairs={{0,4},{2,6},{4,0},{6,2},{1,5},{3,7},{5,1},{7,3},{8,12},{10,14},{12... | collective-permute-start | bytes 6635528 | tf_op jit(solution)/shard_map/ppermute | solution.py:123
  184.5 94.1 %collective-permute-start.4 = (bf16[4,320,864]{2,1,0:T(8,128)(2,1)S(1)}, bf16[4,320,864]{2,1,0:T(8,128)(2,1)S(1)}, u32[]{:S(2)}, u32[]{:S(2)}) collective-permute-start(bf16[4,320,864]{2,1,0:T(8,128)(2,1)S(1)} %shard_map.148.refs_0_), channel_id=1, source_target_pairs={{0,2},{2,0},{4,6},{6,4},{1,3},{3,1},{5,7},{7,5},{8,10},{10,8},{12,... | collective-permute-start | bytes 6635528 | tf_op jit(solution)/shard_map/ppermute | solution.py:123
  185.8 94.3 %collective-permute-start.17 = (bf16[320,864]{1,0:T(8,128)(2,1)S(1)}, bf16[320,864]{1,0:T(8,128)(2,1)S(1)}, u32[]{:S(2)}, u32[]{:S(2)}) collective-permute-start(bf16[320,864]{1,0:T(8,128)(2,1)S(1)} %get-tuple-element.68), channel_id=1, source_target_pairs={{0,24},{8,0},{16,8},{24,16},{1,25},{9,1},{17,9},{25,17},{2,26},{10... | collective-permute-start | bytes 1658888 | tf_op jit(solution)/shard_map/ppermute | solution.py:104
  221.8 62.1 %collective-permute-start.15 = (bf16[320,864]{1,0:T(8,128)(2,1)S(1)}, bf16[320,864]{1,0:T(8,128)(2,1)S(1)}, u32[]{:S(2)}, u32[]{:S(2)}) collective-permute-start(bf16[320,864]{1,0:T(8,128)(2,1)S(1)} %get-tuple-element.69), channel_id=1, source_target_pairs={{0,8},{8,16},{16,24},{24,0},{1,9},{9,17},{17,25},{25,1},{2,10},{10... | collective-permute-start | bytes 1658888 | tf_op jit(solution)/shard_map/ppermute | solution.py:104
  229.4 73.7 %collective-permute-start.14 = (bf16[2,320,864]{2,1,0:T(8,128)(2,1)S(1)}, bf16[2,320,864]{2,1,0:T(8,128)(2,1)S(1)}, u32[]{:S(2)}, u32[]{:S(2)}) collective-permute-start(bf16[2,320,864]{2,1,0:T(8,128)(2,1)S(1)} %slice.185), channel_id=1, source_target_pairs={{0,2},{2,0},{4,6},{6,4},{1,3},{3,1},{5,7},{7,5},{8,10},{10,8},{12,... | collective-permute-start | bytes 3317768 | tf_op jit(solution)/shard_map/ppermute | solution.py:134
  270.0 34.4 %collective-permute-start.12 = (bf16[2,320,864]{2,1,0:T(8,128)(2,1)}, bf16[2,320,864]{2,1,0:T(8,128)(2,1)S(1)}, u32[]{:S(2)}, u32[]{:S(2)}) collective-permute-start(bf16[2,320,864]{2,1,0:T(8,128)(2,1)} %slice.184), channel_id=1, source_target_pairs={{0,4},{2,6},{4,0},{6,2},{1,5},{3,7},{5,1},{7,3},{8,12},{10,14},{12... | collective-permute-start | bytes 3317768 | tf_op jit(solution)/shard_map/ppermute | solution.py:134
  278.6 47.3 %collective-permute-start.7 = (bf16[2,320,864]{2,1,0:T(8,128)(2,1)S(1)}, bf16[2,320,864]{2,1,0:T(8,128)(2,1)S(1)}, u32[]{:S(2)}, u32[]{:S(2)}) collective-permute-start(bf16[2,320,864]{2,1,0:T(8,128)(2,1)S(1)} %slice.183), channel_id=1, source_target_pairs={{0,2},{2,0},{4,6},{6,4},{1,3},{3,1},{5,7},{7,5},{8,10},{10,8},{12,... | collective-permute-start | bytes 3317768 | tf_op jit(solution)/shard_map/ppermute | solution.py:134
  280.2 47.3 %collective-permute-start.5 = (bf16[2,320,864]{2,1,0:T(8,128)(2,1)S(1)}, bf16[2,320,864]{2,1,0:T(8,128)(2,1)S(1)}, u32[]{:S(2)}, u32[]{:S(2)}) collective-permute-start(bf16[2,320,864]{2,1,0:T(8,128)(2,1)S(1)} %slice.182), channel_id=1, source_target_pairs={{0,4},{2,6},{4,0},{6,2},{1,5},{3,7},{5,1},{7,3},{8,12},{10,14},{12... | collective-permute-start | bytes 3317768 | tf_op jit(solution)/shard_map/ppermute | solution.py:134
  283.9 11.7 %collective-permute-start.16 = (bf16[320,864]{1,0:T(8,128)(2,1)S(1)}, bf16[320,864]{1,0:T(8,128)(2,1)S(1)}, u32[]{:S(2)}, u32[]{:S(2)}) collective-permute-start(bf16[320,864]{1,0:T(8,128)(2,1)S(1)} %get-tuple-element.71), channel_id=1, source_target_pairs={{0,16},{8,24},{16,0},{24,8},{1,17},{9,25},{17,1},{25,9},{2,18},{10... | collective-permute-start | bytes 1658888 | tf_op jit(solution)/shard_map/ppermute | solution.py:104
  295.6 91.9 %collective-permute-start.24 = (bf16[256,5120]{1,0:T(8,128)(2,1)}, bf16[256,5120]{1,0:T(8,128)(2,1)}, u32[]{:S(2)}, u32[]{:S(2)}) collective-permute-start(bf16[256,5120]{1,0:T(8,128)(2,1)} %broadcast_select_fusion.1.own), channel_id=1, source_target_pairs={{0,1},{1,0},{2,3},{3,2},{4,5},{5,4},{6,7},{7,6},{8,9},{9,8},{10,11... | collective-permute-start | bytes 7864328 | tf_op jit(solution)/shard_map/ppermute | solution.py:186
  303.2 108.3 %collective-permute-start.25 = (bf16[256,5120]{1,0:T(8,128)(2,1)}, bf16[256,5120]{1,0:T(8,128)(2,1)}, u32[]{:S(2)}, u32[]{:S(2)}) collective-permute-start(bf16[256,5120]{1,0:T(8,128)(2,1)} %collective-permute-done.19), channel_id=1, source_target_pairs={{8,0},{16,8},{9,1},{17,9},{10,2},{18,10},{11,3},{19,11},{12,4},{20... | collective-permute-start | bytes 7864328 | tf_op jit(solution)/shard_map/ppermute | solution.py:163
  304.5 107.0 %collective-permute-start.26 = (bf16[256,5120]{1,0:T(8,128)(2,1)}, bf16[256,5120]{1,0:T(8,128)(2,1)}, u32[]{:S(2)}, u32[]{:S(2)}) collective-permute-start(bf16[256,5120]{1,0:T(8,128)(2,1)} %collective-permute-done.18), channel_id=1, source_target_pairs={{8,16},{16,24},{9,17},{17,25},{10,18},{18,26},{11,19},{19,27},{12,... | collective-permute-start | bytes 7864328 | tf_op jit(solution)/shard_map/ppermute | solution.py:162
  325.9 50.3 %collective-permute-start.22 = (bf16[4,320,864]{2,1,0:T(8,128)(2,1)S(1)}, bf16[4,320,864]{2,1,0:T(8,128)(2,1)}, u32[]{:S(2)}, u32[]{:S(2)}) collective-permute-start(bf16[4,320,864]{2,1,0:T(8,128)(2,1)S(1)} %shard_map.154.refs_0_), channel_id=1, source_target_pairs={{0,4},{2,6},{4,0},{6,2},{1,5},{3,7},{5,1},{7,3},{8,12},{10,14},{12... | collective-permute-start | bytes 6635528 | tf_op jit(solution)/shard_map/ppermute | solution.py:123
  327.5 52.6 %collective-permute-start.20 = (bf16[4,320,864]{2,1,0:T(8,128)(2,1)S(1)}, bf16[4,320,864]{2,1,0:T(8,128)(2,1)}, u32[]{:S(2)}, u32[]{:S(2)}) collective-permute-start(bf16[4,320,864]{2,1,0:T(8,128)(2,1)S(1)} %shard_map.154.refs_0_), channel_id=1, source_target_pairs={{0,2},{2,0},{4,6},{6,4},{1,3},{3,1},{5,7},{7,5},{8,10},{10,8},{12,... | collective-permute-start | bytes 6635528 | tf_op jit(solution)/shard_map/ppermute | solution.py:123
  378.6 43.1 %collective-permute-start.23 = (bf16[2,320,864]{2,1,0:T(8,128)(2,1)}, bf16[2,320,864]{2,1,0:T(8,128)(2,1)}, u32[]{:S(2)}, u32[]{:S(2)}) collective-permute-start(bf16[2,320,864]{2,1,0:T(8,128)(2,1)} %slice.187), channel_id=1, source_target_pairs={{0,2},{2,0},{4,6},{6,4},{1,3},{3,1},{5,7},{7,5},{8,10},{10,8},{12,... | collective-permute-start | bytes 3317768 | tf_op jit(solution)/shard_map/ppermute | solution.py:134
  382.4 39.3 %collective-permute-start.21 = (bf16[2,320,864]{2,1,0:T(8,128)(2,1)}, bf16[2,320,864]{2,1,0:T(8,128)(2,1)}, u32[]{:S(2)}, u32[]{:S(2)}) collective-permute-start(bf16[2,320,864]{2,1,0:T(8,128)(2,1)} %slice.186), channel_id=1, source_target_pairs={{0,4},{2,6},{4,0},{6,2},{1,5},{3,7},{5,1},{7,3},{8,12},{10,14},{12... | collective-permute-start | bytes 3317768 | tf_op jit(solution)/shard_map/ppermute | solution.py:134
  413.9 31.5 %collective-permute-start.27 = (bf16[256,5120]{1,0:T(8,128)(2,1)S(1)}, bf16[256,5120]{1,0:T(8,128)(2,1)}, u32[]{:S(2)}, u32[]{:S(2)}) collective-permute-start(bf16[256,5120]{1,0:T(8,128)(2,1)S(1)} %broadcast_select_fusion.own), channel_id=1, source_target_pairs={{0,1},{1,0},{2,3},{3,2},{4,5},{5,4},{6,7},{7,6},{8,9},{9,8},{10,11... | collective-permute-start | bytes 7864328 | tf_op jit(solution)/shard_map/ppermute | solution.py:186
  413.9 61.5 %collective-permute-start.28 = (bf16[256,5120]{1,0:T(8,128)(2,1)}, bf16[256,5120]{1,0:T(8,128)(2,1)}, u32[]{:S(2)}, u32[]{:S(2)}) collective-permute-start(bf16[256,5120]{1,0:T(8,128)(2,1)} %collective-permute-done.25), channel_id=1, source_target_pairs={{8,0},{9,1},{10,2},{11,3},{12,4},{13,5},{14,6},{15,7}} | collective-permute-start | bytes 7864328 | tf_op jit(solution)/shard_map/ppermute | solution.py:163
  415.2 60.2 %collective-permute-start.29 = (bf16[256,5120]{1,0:T(8,128)(2,1)}, bf16[256,5120]{1,0:T(8,128)(2,1)}, u32[]{:S(2)}, u32[]{:S(2)}) collective-permute-start(bf16[256,5120]{1,0:T(8,128)(2,1)} %collective-permute-done.26), channel_id=1, source_target_pairs={{16,24},{17,25},{18,26},{19,27},{20,28},{21,29},{22,30},{23,31}} | collective-permute-start | bytes 7864328 | tf_op jit(solution)/shard_map/ppermute | solution.py:162
  477.8 28.6 %collective-permute-start.30 = (bf16[256,5120]{1,0:T(8,128)(2,1)S(1)}, bf16[256,5120]{1,0:T(8,128)(2,1)}, u32[]{:S(2)}, u32[]{:S(2)}) collective-permute-start(bf16[256,5120]{1,0:T(8,128)(2,1)S(1)} %select_select_fusion.own), channel_id=1, source_target_pairs={{0,1},{1,0},{2,3},{3,2},{4,5},{5,4},{6,7},{7,6},{8,9},{9,8},{10,11... | collective-permute-start | bytes 7864328 | tf_op jit(solution)/shard_map/ppermute | solution.py:186
  (62 other events, 740.2 us)
